TPU v7x, 32 devices: a 4x2x2 block of a 4x4x8 slice. The times are simulated.
32 devices in a mesh: dp: 4 (over y, z), tp: 8 (over x, core).
Axes of the slice: x: 4, y: 2, z: 2, core: 2. Of those that a mesh axis runs over, the one named last changes fastest.
The devices are a block of a 4x4x8 slice.
Arguments:
- x: bfloat16 [4, 2048, 1024], P('dp', 'tp'), parts along dimension 0
- ln1_gamma: float32 [1024], replicated
- ln1_beta: float32 [1024], replicated
- w_qkv: bfloat16 [1024, 16, 3, 64], P(None, 'tp')
- b_qkv: float32 [16, 3, 64], P('tp')
- w_out: bfloat16 [1024, 1024], P('tp')
- b_out: float32 [1024], replicated
- ln2_gamma: float32 [1024], replicated
- ln2_beta: float32 [1024], replicated
- w_up: bfloat16 [1024, 4096], P(None, 'tp')
- b_up: float32 [4096], P('tp')
- w_down: bfloat16 [4096, 1024], P('tp')
- b_down: float32 [1024], replicated
- grad_y: bfloat16 [4, 2048, 1024], P('dp', 'tp'), parts along dimension 0
Outputs:
- output 1: bfloat16 [4, 2048, 1024], P('dp', 'tp'), parts along dimension 0
- output 2: bfloat16 [4, 2048, 1024], P('dp', 'tp'), parts along dimension 0
- output 3: float32 [4096], P('dp'), parts along dimension 0
- output 4: float32 [4096], P('dp'), parts along dimension 0
- output 5: bfloat16 [4096, 16, 3, 64], P('dp', 'tp'), parts along dimension 0
- output 6: float32 [64, 3, 64], P(('dp', 'tp')), parts along dimension 0
- output 7: bfloat16 [4096, 1024], P(('dp', 'tp')), parts along dimension 0
- output 8: float32 [4096], P('dp'), parts along dimension 0
- output 9: float32 [4096], P('dp'), parts along dimension 0
- output 10: float32 [4096], P('dp'), parts along dimension 0
- output 11: bfloat16 [4096, 4096], P('dp', 'tp'), parts along dimension 0
- output 12: float32 [16384], P(('dp', 'tp')), parts along dimension 0
- output 13: bfloat16 [16384, 1024], P(('dp', 'tp')), parts along dimension 0
- output 14: float32 [4096], P('dp'), parts along dimension 0
There are 4 independent parts. A program takes and returns all parts, laid end to end along the dimension named above; an argument that names none is the same for every part.
All inputs are finite; a program needn't handle non-finite values.
Results may differ from a plain program's by a relative error of at most 0.02.
Values are sent between devices in bfloat16 or wider.
A program may use at most 768 MiB of HBM per device.

v0:
```python
import math
import jax
import jax.numpy as jnp
from jax import lax
from jax.sharding import PartitionSpec as P

EPS = 1e-5
MASK_VALUE = -1e30


def alibi_slopes(n_heads):
    closest = 2 ** int(math.floor(math.log2(n_heads)))
    base_ratio = 2.0 ** (-8.0 / closest)
    extra_ratio = 2.0 ** (-4.0 / closest)
    remaining = min(closest, n_heads - closest)
    slopes = [base_ratio ** (i + 1) for i in range(closest)]
    slopes = slopes + [extra_ratio ** (2 * i + 1) for i in range(remaining)]
    return jnp.array(slopes, dtype=jnp.float32)


def layer_norm(values, ln_gain, ln_bias):
    row_mean = jnp.mean(values, axis=-1, keepdims=True)
    centered = values - row_mean
    variance = jnp.mean(centered * centered, axis=-1, keepdims=True)
    return centered * lax.rsqrt(variance + EPS) * ln_gain + ln_bias


def gelu_tanh(values):
    return jax.nn.gelu(values, approximate=True)


def seq_gather(values):
    return lax.all_gather(values, 'tp', axis=1, tiled=True)


def seq_reduce(values):
    return lax.psum_scatter(values, 'tp', scatter_dimension=1, tiled=True)


def solution(mesh):
    tp_size = mesh.shape['tp']

    def local_step(x, ln1_gamma, ln1_beta, w_qkv, b_qkv, w_out, b_out, ln2_gamma, ln2_beta, w_up, b_up, w_down, b_down, grad_y):
        batch_size, seq_local = x.shape[0], x.shape[1]
        local_heads, head_size = w_qkv.shape[1], w_qkv.shape[3]
        seq_full = seq_local * tp_size
        score_scale = head_size ** -0.5
        tp_index = lax.axis_index('tp')
        slopes = lax.dynamic_slice_in_dim(alibi_slopes(local_heads * tp_size), tp_index * local_heads, local_heads)
        positions = jnp.arange(seq_full)
        causal = positions[None, :] <= positions[:, None]
        alibi_bias = slopes[:, None] * positions.astype(jnp.float32)[None, :]

        x_f = x.astype(jnp.float32)
        h_full = seq_gather(layer_norm(x_f, ln1_gamma, ln1_beta).astype(jnp.bfloat16))
        qkv_vals = (jnp.einsum('bsd,dhte->bshte', h_full, w_qkv, preferred_element_type=jnp.float32) + b_qkv).astype(jnp.bfloat16)
        q_heads = qkv_vals[:, :, :, 0]
        k_heads = qkv_vals[:, :, :, 1]
        v_heads = qkv_vals[:, :, :, 2]
        scores = jnp.einsum('bihe,bjhe->bhij', q_heads, k_heads, preferred_element_type=jnp.float32) * score_scale + alibi_bias[None, :, None, :]
        prob_f = jax.nn.softmax(jnp.where(causal, scores, MASK_VALUE), axis=-1)
        prob_bf = prob_f.astype(jnp.bfloat16)
        context = jnp.einsum('bhij,bjhe->bihe', prob_bf, v_heads, preferred_element_type=jnp.float32).astype(jnp.bfloat16)
        context_flat = context.reshape(batch_size, seq_full, local_heads * head_size)
        attn_out = seq_reduce(jnp.einsum('bsc,cd->bsd', context_flat, w_out, preferred_element_type=jnp.float32).astype(jnp.bfloat16))
        x_mid = x_f + attn_out.astype(jnp.float32) + b_out
        g_full = seq_gather(layer_norm(x_mid, ln2_gamma, ln2_beta).astype(jnp.bfloat16))
        pre_act = jnp.einsum('bsd,df->bsf', g_full, w_up, preferred_element_type=jnp.float32) + b_up
        activated = gelu_tanh(pre_act).astype(jnp.bfloat16)
        mlp_out = seq_reduce(jnp.einsum('bsf,fd->bsd', activated, w_down, preferred_element_type=jnp.float32).astype(jnp.bfloat16))
        y = (x_mid + mlp_out.astype(jnp.float32) + b_down).astype(jnp.bfloat16)

        grad_y_f = grad_y.astype(jnp.float32)
        grad_b_down = lax.psum(jnp.sum(grad_y_f, axis=(0, 1)), 'tp')
        grad_m_full = seq_gather(grad_y)
        grad_w_down = jnp.einsum('bsf,bsd->fd', activated, grad_m_full, preferred_element_type=jnp.float32).astype(jnp.bfloat16)
        grad_act = jnp.einsum('bsd,fd->bsf', grad_m_full, w_down, preferred_element_type=jnp.float32).astype(jnp.bfloat16)
        _, gelu_pullback = jax.vjp(gelu_tanh, pre_act)
        grad_pre = gelu_pullback(grad_act.astype(jnp.float32))[0]
        grad_b_up = jnp.sum(grad_pre, axis=(0, 1))
        grad_pre_bf = grad_pre.astype(jnp.bfloat16)
        grad_w_up = jnp.einsum('bsd,bsf->df', g_full, grad_pre_bf, preferred_element_type=jnp.float32).astype(jnp.bfloat16)
        grad_g = seq_reduce(jnp.einsum('bsf,df->bsd', grad_pre_bf, w_up, preferred_element_type=jnp.float32).astype(jnp.bfloat16))
        _, ln2_pullback = jax.vjp(layer_norm, x_mid, ln2_gamma, ln2_beta)
        grad_mid_ln, grad_ln2_gamma, grad_ln2_beta = ln2_pullback(grad_g.astype(jnp.float32))
        grad_ln2_gamma = lax.psum(grad_ln2_gamma, 'tp')
        grad_ln2_beta = lax.psum(grad_ln2_beta, 'tp')
        grad_mid = grad_y_f + grad_mid_ln
        grad_b_out = lax.psum(jnp.sum(grad_mid, axis=(0, 1)), 'tp')
        grad_attn_full = seq_gather(grad_mid.astype(jnp.bfloat16))
        grad_w_out = jnp.einsum('bsc,bsd->cd', context_flat, grad_attn_full, preferred_element_type=jnp.float32).astype(jnp.bfloat16)
        grad_context = jnp.einsum('bsd,cd->bsc', grad_attn_full, w_out, preferred_element_type=jnp.float32).astype(jnp.bfloat16)
        grad_context = grad_context.reshape(batch_size, seq_full, local_heads, head_size)
        grad_prob = jnp.einsum('bihe,bjhe->bhij', grad_context, v_heads, preferred_element_type=jnp.float32).astype(jnp.bfloat16).astype(jnp.float32)
        grad_v = jnp.einsum('bhij,bihe->bjhe', prob_bf, grad_context, preferred_element_type=jnp.float32).astype(jnp.bfloat16)
        grad_scores = prob_f * (grad_prob - jnp.sum(grad_prob * prob_f, axis=-1, keepdims=True))
        grad_scores_bf = grad_scores.astype(jnp.bfloat16)
        grad_q = (jnp.einsum('bhij,bjhe->bihe', grad_scores_bf, k_heads, preferred_element_type=jnp.float32) * score_scale).astype(jnp.bfloat16)
        grad_k = (jnp.einsum('bhij,bihe->bjhe', grad_scores_bf, q_heads, preferred_element_type=jnp.float32) * score_scale).astype(jnp.bfloat16)
        grad_qkv = jnp.stack([grad_q, grad_k, grad_v], axis=3)
        grad_b_qkv = jnp.sum(grad_qkv, axis=(0, 1), dtype=jnp.float32)
        grad_w_qkv = jnp.einsum('bsd,bshte->dhte', h_full, grad_qkv, preferred_element_type=jnp.float32).astype(jnp.bfloat16)
        grad_h = seq_reduce(jnp.einsum('bshte,dhte->bsd', grad_qkv, w_qkv, preferred_element_type=jnp.float32).astype(jnp.bfloat16))
        _, ln1_pullback = jax.vjp(layer_norm, x_f, ln1_gamma, ln1_beta)
        grad_x_ln, grad_ln1_gamma, grad_ln1_beta = ln1_pullback(grad_h.astype(jnp.float32))
        grad_ln1_gamma = lax.psum(grad_ln1_gamma, 'tp')
        grad_ln1_beta = lax.psum(grad_ln1_beta, 'tp')
        grad_x = (grad_mid + grad_x_ln).astype(jnp.bfloat16)
        return (y, grad_x, grad_ln1_gamma, grad_ln1_beta, grad_w_qkv, grad_b_qkv, grad_w_out, grad_b_out,
                grad_ln2_gamma, grad_ln2_beta, grad_w_up, grad_b_up, grad_w_down, grad_b_down)

    row_spec = P('dp', 'tp', None)
    in_specs = (row_spec, P(), P(), P(None, 'tp', None, None), P('tp', None, None), P('tp', None), P(), P(), P(),
                P(None, 'tp'), P('tp'), P('tp', None), P(), row_spec)
    out_specs = (row_spec, row_spec, P('dp'), P('dp'), P('dp', 'tp', None, None), P(('dp', 'tp'), None, None),
                 P(('dp', 'tp'), None), P('dp'), P('dp'), P('dp'), P('dp', 'tp'), P(('dp', 'tp')), P(('dp', 'tp'), None), P('dp'))
    return jax.shard_map(local_step, mesh=mesh, in_specs=in_specs, out_specs=out_specs, check_vma=False)
```

profile of v0, /device:TPU:80, one launch (start us, length us, event | category | flops | bytes accessed | tf_op | source)
XLA Modules:
  0.0 447.9 jit_solution(14736386335124171814)
XLA Ops:
  14.9 4.2 iota_compare_fusion
  19.0 25.9 %all-gather.5.cloned.1.call-done = bf16[1,2048,1024]{2,1,0:T(8,128)(2,1)} async-done(((bf16[1,256,1024]{2,1,0:T(8,128)(2,1)}), bf16[1,2048,1024]{2,1,0:T(8,128)(2,1)}) %all-gather.5.cloned.1.call-update) | async-done | bytes 4194320 | tf_op jit(solution)/shard_map/all_gather | solution.py:33
  49.3 19.7 %fusion.102 = (f32[2,2048]{1,0:T(2,128)S(1)}, f32[2,2048,2048]{1,2,0:T(8,128)}) fusion(f32[2,2048]{1,0:T(2,128)S(1)} %broadcast_multiply_fusion, pred[2048,2048]{0,1:T(8,128)(4,1)} %iota_compare_fusion, bf16[1,2048,2,3,64]{1,4,3,2,0:T(8,128)(2,1)S(1)} %fusion.62), kind=kOutput, calls=%fused_computation.134 | convolution fusion | flops 1115686912 | bytes 38830080 | tf_op jit(solution)/shard_map/sub | solution.py:61
  69.0 12.3 %fusion.44 = bf16[2,64,2048]{2,1,0:T(8,128)(2,1)S(1)} fusion(bf16[1,2048,2,3,64]{1,4,3,2,0:T(8,128)(2,1)S(1)} %fusion.62, f32[2,2048,2048]{1,2,0:T(8,128)} %get-tuple-element.33, f32[2,2048]{1,0:T(2,128)S(1)} %get-tuple-element.32), kind=kOutput, calls=%fused_computation.61 | convolution fusion | flops 1090781184 | bytes 34619392 | tf_op jit(solution)/shard_map/bhij,bjhe->bihe/dot_general | solution.py:63
  85.5 34.9 %reduce-scatter.5.cloned.1.call-done = bf16[1,256,1024]{2,1,0:T(8,128)(2,1)} async-done(((bf16[1,2048,1024]{2,1,0:T(8,128)(2,1)}), bf16[1,256,1024]{2,1,0:T(8,128)(2,1)}) %reduce-scatter.5.cloned.1.call-update) | async-done | bytes 524304 | tf_op jit(solution)/shard_map/reduce_scatter | solution.py:37
  126.2 26.8 %all-gather.7.cloned.1.call-done = bf16[1,2048,1024]{2,1,0:T(8,128)(2,1)} async-done(((bf16[1,256,1024]{2,1,0:T(8,128)(2,1)}), bf16[1,2048,1024]{2,1,0:T(8,128)(2,1)}) %all-gather.7.cloned.1.call-update) | async-done | bytes 4194320 | tf_op jit(solution)/shard_map/all_gather | solution.py:33
  153.0 6.7 %fusion.32 = f32[2048,512]{1,0:T(8,128)} fusion(bf16[1024,512]{1,0:T(8,128)(2,1)} %param.24, bf16[1,2048,1024]{2,1,0:T(8,128)(2,1)} %all-gather.7.cloned.1.call-done), kind=kOutput, calls=%fused_computation.44 | convolution fusion | flops 2147483648 | bytes 9437184 | tf_op jit(solution)/shard_map/bsd,df->bsf/dot_general | solution.py:68
  159.8 23.4 %all-gather.9.cloned.1.call-done = bf16[1,2048,1024]{2,1,0:T(8,128)(2,1)} async-done(((bf16[1,256,1024]{2,1,0:T(8,128)(2,1)}), bf16[1,2048,1024]{2,1,0:T(8,128)(2,1)}) %all-gather.9.cloned.1.call-update) | async-done | bytes 4194320 | tf_op jit(solution)/shard_map/all_gather | solution.py:33
  183.2 8.4 %fusion.103 = (f32[512]{0:T(512)}, bf16[2048,512]{1,0:T(8,128)(2,1)S(1)}) fusion(f32[2048,512]{1,0:T(8,128)} %fusion.32, f32[512]{0:T(512)S(1)} %copy-done.38, bf16[512,1024]{1,0:T(8,128)(2,1)S(1)} %copy-done, bf16[1,2048,1024]{2,1,0:T(8,128)(2,1)} %all-gather.9.cloned.1.call-done), kind=kOutput, calls=%fused_computation.135 | convolution fusion | flops 2172648960 | bytes 11538432 | tf_op jit(solution)/shard_map/bsd,fd->bsf/dot_general | solution.py:77
  192.9 4.4 convert_bitcast_fusion
  197.5 7.1 %convert_bitcast_fusion.1 = bf16[1,2048,1024]{2,1,0:T(8,128)(2,1)} fusion(bf16[512,1024]{1,0:T(8,128)(2,1)S(1)} %copy-done, f32[2048,512]{1,0:T(8,128)} %fusion.32, f32[512]{0:T(512)S(1)} %copy-done.38), kind=kOutput, calls=%fused_computation.51 | convolution fusion | flops 2160066560 | bytes 9439232 | tf_op jit(solution)/shard_map/bsf,fd->bsd/dot_general | solution.py:70
  204.7 27.7 %reduce-scatter.9.cloned.1.call-done = bf16[1,256,1024]{2,1,0:T(8,128)(2,1)} async-done(((bf16[1,2048,1024]{2,1,0:T(8,128)(2,1)}), bf16[1,256,1024]{2,1,0:T(8,128)(2,1)}) %reduce-scatter.9.cloned.1.call-update) | async-done | bytes 524304 | tf_op jit(solution)/shard_map/reduce_scatter | solution.py:37
  236.8 31.5 %reduce-scatter.7.cloned.1.call-done = bf16[1,256,1024]{2,1,0:T(8,128)(2,1)} async-done(((bf16[1,2048,1024]{2,1,0:T(8,128)(2,1)}), bf16[1,256,1024]{2,1,0:T(8,128)(2,1)}) %reduce-scatter.7.cloned.1.call-update) | async-done | bytes 524304 | tf_op jit(solution)/shard_map/reduce_scatter | solution.py:37
  273.6 27.7 %all-gather.11.cloned.1.call-done = bf16[1,2048,1024]{2,1,0:T(8,128)(2,1)} async-done(((bf16[1,256,1024]{2,1,0:T(8,128)(2,1)}), bf16[1,2048,1024]{2,1,0:T(8,128)(2,1)}) %all-gather.11.cloned.1.call-update) | async-done | bytes 4194320 | tf_op jit(solution)/shard_map/all_gather | solution.py:33
  305.7 13.3 %fusion.57 = bf16[1,2048,2,1,64]{1,4,2,3,0:T(8,128)(2,1)S(1)} fusion(bf16[2048,2,64]{0,2,1:T(8,128)(2,1)S(1)} %bitcast.135, f32[2,2048,2048]{1,2,0:T(8,128)} %get-tuple-element.33, f32[2,2048]{1,0:T(2,128)S(1)} %get-tuple-element.32), kind=kOutput, calls=%fused_computation.68 | convolution fusion | flops 1090781184 | bytes 34619392 | tf_op jit(solution)/shard_map/bhij,bihe->bjhe/dot_general | solution.py:95
  319.0 12.5 %fusion.1 = (f32[2,2048]{1,0:T(2,128)S(1)}, bf16[2,2048,2048]{1,2,0:T(8,128)(2,1)S(1)}) fusion(f32[2,2048,2048]{1,2,0:T(8,128)} %get-tuple-element.33, f32[2,2048]{1,0:T(2,128)S(1)} %get-tuple-element.32, bf16[2048,2,64]{0,2,1:T(8,128)(2,1)} %bitcast.136, bf16[1,2048,2,3,64]{1,4,3,2,0:T(8,128)(2,1)S(1)} %fusion.62), kind=kOutput, calls=%fused_computation.3 | convolution fusion | flops 1115680768 | bytes 51412992 | tf_op jit(solution)/shard_map/bihe,bjhe->bhij/dot_general | solution.py:94
  331.5 19.7 %fusion.3 = bf16[2,2048,2048]{1,2,0:T(8,128)(2,1)} fusion(bf16[2,2048,2048]{1,2,0:T(8,128)(2,1)S(1)} %get-tuple-element.35, f32[2,2048]{1,0:T(2,128)S(1)} %get-tuple-element.34, f32[2,2048,2048]{1,2,0:T(8,128)} %get-tuple-element.33, f32[2,2048]{1,0:T(2,128)S(1)} %get-tuple-element.32), kind=kLoop, calls=%fused_computation.5 | loop fusion | flops 41943040 | bytes 67141632 | tf_op jit(solution)/shard_map/convert_element_type | solution.py:97
  351.2 11.0 %fusion.55 = bf16[1,2048,2,1,64]{1,4,2,3,0:T(8,128)(2,1)S(1)} fusion(bf16[2,2048,2048]{1,2,0:T(8,128)(2,1)} %fusion.3, bf16[1,2048,2,3,64]{1,4,3,2,0:T(8,128)(2,1)S(1)} %fusion.62), kind=kOutput, calls=%fused_computation.66 | convolution fusion | flops 1074266112 | bytes 17825792 | tf_op jit(solution)/shard_map/bhij,bihe->bjhe/dot_general | solution.py:99
  362.2 9.0 %fusion.56 = bf16[1,2048,2,1,64]{1,4,2,3,0:T(8,128)(2,1)S(1)} fusion(bf16[2,2048,2048]{1,2,0:T(8,128)(2,1)} %fusion.3, bf16[1,2048,2,3,64]{1,4,3,2,0:T(8,128)(2,1)S(1)} %fusion.62), kind=kOutput, calls=%fused_computation.67 | convolution fusion | flops 1074266112 | bytes 17825792 | tf_op jit(solution)/shard_map/bhij,bjhe->bihe/dot_general | solution.py:98
  371.2 4.3 fusion.40
  375.6 6.3 %fusion.67 = bf16[1024,512]{1,0:T(8,128)(2,1)} fusion(bf16[1,2048,1024]{2,1,0:T(8,128)(2,1)} %all-gather.7.cloned.1.call-done, bf16[2048,512]{1,0:T(8,128)(2,1)} %copy-done.40), kind=kOutput, calls=%fused_computation.86 | convolution fusion | flops 2148007936 | bytes 7340032 | tf_op jit(solution)/shard_map/bsd,bsf->df/dot_general | solution.py:82
  382.0 6.0 %fusion.70 = bf16[512,1024]{1,0:T(8,128)(2,1)} fusion(bf16[1,2048,1024]{2,1,0:T(8,128)(2,1)S(1)} %copy-done.34, f32[2048,512]{1,0:T(8,128)} %fusion.32, f32[512]{0:T(512)S(1)} %copy-done.38), kind=kOutput, calls=%fused_computation.87 | convolution fusion | flops 2158493696 | bytes 9439232 | tf_op jit(solution)/shard_map/bsf,bsd->fd/dot_general | solution.py:76
  395.4 15.2 %reduce-scatter.11.cloned.1.call-done = bf16[1,256,1024]{2,1,0:T(8,128)(2,1)} async-done(((bf16[1,2048,1024]{2,1,0:T(8,128)(2,1)}), bf16[1,256,1024]{2,1,0:T(8,128)(2,1)}) %reduce-scatter.11.cloned.1.call-update) | async-done | bytes 524304 | tf_op jit(solution)/shard_map/reduce_scatter | solution.py:37
  413.7 24.6 %all-reduce = (f32[1024]{0:T(1024)}, f32[1024]{0:T(1024)}, f32[1024]{0:T(1024)}, f32[1024]{0:T(1024)}, f32[1024]{0:T(1024)}, /*index=5*/f32[1024]{0:T(1024)}) all-reduce(f32[1024]{0:T(1024)S(1)} %get-tuple-element.16, f32[1024]{0:T(1024)S(1)} %get-tuple-element.20, f32[1024]{0:T(1024)S(1)} %copy-done.27, ...), channel_id=1, replica_groups=mesh['dp'=4,'tp'=8] {'tp'}, use_global_device_ids=true, to_apply=%region_16.17 | all-reduce | flops 6144 | bytes 49152 | tf_op jit(solution)/shard_map/psum | solution.py:106
  (133 shorter events, 50.4 us)
Async XLA Ops:
  7.2 176.0 %copy-start = (bf16[512,1024]{1,0:T(8,128)(2,1)S(1)}, bf16[512,1024]{1,0:T(8,128)(2,1)}, u32[]{:S(2)}) copy-start(bf16[512,1024]{1,0:T(8,128)(2,1)} %param.26) | copy-start | bytes 3145732
  7.2 37.8 %copy-start.36 = (bf16[1024,2,3,64]{0,3,2,1:T(8,128)(2,1)S(1)}, bf16[1024,2,3,64]{0,3,2,1:T(8,128)(2,1)}, u32[]{:S(2)}) copy-start(bf16[1024,2,3,64]{0,3,2,1:T(8,128)(2,1)} %param.18) | copy-start | bytes 2359300
  7.2 37.7 %all-gather.5.cloned.1.call-start = ((), (), s32[]{:S(2)}) async-start(), calls=%async_computation.4 | async-start | bytes 4718592 | tf_op jit(solution)/shard_map/all_gather | solution.py:33
  13.3 107.1 %reduce-scatter.5.cloned.1.call-start = ((), (), s32[]{:S(2)}) async-start(), calls=%async_computation.5 | async-start | bytes 4718592 | tf_op jit(solution)/shard_map/reduce_scatter | solution.py:37
  82.0 38.3 %copy-start.2 = (bf16[1,256,1024]{2,1,0:T(8,128)(2,1)S(1)}, bf16[1,256,1024]{2,1,0:T(8,128)(2,1)}, u32[]{:S(2)}) copy-start(bf16[1,256,1024]{2,1,0:T(8,128)(2,1)} %param.15) | copy-start | bytes 1572868
  82.0 38.3 %copy-start.18 = (f32[1024]{0:T(1024)S(1)}, f32[1024]{0:T(1024)}, u32[]{:S(2)}) copy-start(f32[1024]{0:T(1024)} %param.21) | copy-start | bytes 12292
  85.4 37.7 %copy-start.20 = (f32[1024]{0:T(1024)S(1)}, f32[1024]{0:T(1024)}, u32[]{:S(2)}) copy-start(f32[1024]{0:T(1024)} %param.22) | copy-start | bytes 12292
  85.4 37.7 %copy-start.31 = (f32[1024]{0:T(1024)S(1)}, f32[1024]{0:T(1024)}, u32[]{:S(2)}) copy-start(f32[1024]{0:T(1024)} %param.23) | copy-start | bytes 12292
  85.4 67.6 %all-gather.7.cloned.1.call-start = ((), (), s32[]{:S(2)}) async-start(), calls=%async_computation.6 | async-start | bytes 4718592 | tf_op jit(solution)/shard_map/all_gather | solution.py:33
  125.3 57.9 %all-gather.9.cloned.1.call-start = ((), (), s32[]{:S(2)}) async-start(), calls=%async_computation.8 | async-start | bytes 4718592 | tf_op jit(solution)/shard_map/all_gather | solution.py:33
  125.9 57.2 %copy-start.38 = (f32[512]{0:T(512)S(1)}, f32[512]{0:T(512)}, u32[]{:S(2)}) copy-start(f32[512]{0:T(512)} %param.25) | copy-start | bytes 6148
  125.9 106.4 %reduce-scatter.9.cloned.1.call-start = ((), (), s32[]{:S(2)}) async-start(), calls=%async_computation.9 | async-start | bytes 4718592 | tf_op jit(solution)/shard_map/reduce_scatter | solution.py:37
  197.4 70.9 %reduce-scatter.7.cloned.1.call-start = ((), (), s32[]{:S(2)}) async-start(), calls=%async_computation.7 | async-start | bytes 4718592 | tf_op jit(solution)/shard_map/reduce_scatter | solution.py:37
  204.5 27.8 %copy-start.4 = (bf16[1,256,1024]{2,1,0:T(8,128)(2,1)S(1)}, bf16[1,256,1024]{2,1,0:T(8,128)(2,1)}, u32[]{:S(2)}) copy-start(bf16[1,256,1024]{2,1,0:T(8,128)(2,1)} %reduce-scatter.5.cloned.1.call-done) | copy-start | bytes 1572868
  204.5 63.8 %copy-start.16 = (bf16[1,256,1024]{2,1,0:T(8,128)(2,1)S(1)}, bf16[1,256,1024]{2,1,0:T(8,128)(2,1)}, u32[]{:S(2)}) copy-start(bf16[1,256,1024]{2,1,0:T(8,128)(2,1)} %param.28) | copy-start | bytes 1572868
  204.5 63.8 %copy-start.32 = (f32[1024]{0:T(1024)S(1)}, f32[1024]{0:T(1024)}, u32[]{:S(2)}) copy-start(f32[1024]{0:T(1024)} %param.27) | copy-start | bytes 12292
  204.6 96.6 %all-gather.11.cloned.1.call-start = ((), (), s32[]{:S(2)}) async-start(), calls=%async_computation.10 | async-start | bytes 4718592 | tf_op jit(solution)/shard_map/all_gather | solution.py:33
  273.5 137.1 %reduce-scatter.11.cloned.1.call-start = ((), (), s32[]{:S(2)}) async-start(), calls=%async_computation.11 | async-start | bytes 4718592 | tf_op jit(solution)/shard_map/reduce_scatter | solution.py:37
  319.0 69.0 %copy-start.14 = (bf16[1,2048,2,1,64]{1,4,2,3,0:T(8,128)(2,1)}, bf16[1,2048,2,1,64]{1,4,2,3,0:T(8,128)(2,1)S(1)}, u32[]{:S(2)}) copy-start(bf16[1,2048,2,1,64]{1,4,2,3,0:T(8,128)(2,1)S(1)} %fusion.57) | copy-start | bytes 1572868
  362.2 25.8 %copy-start.7 = (bf16[1,2048,2,1,64]{1,4,2,3,0:T(8,128)(2,1)}, bf16[1,2048,2,1,64]{1,4,2,3,0:T(8,128)(2,1)S(1)}, u32[]{:S(2)}) copy-start(bf16[1,2048,2,1,64]{1,4,2,3,0:T(8,128)(2,1)S(1)} %fusion.55) | copy-start | bytes 1572868
  393.0 20.7 %copy-start.25 = (f32[1024]{0:T(1024)S(1)}, f32[1024]{0:T(1024)}, u32[]{:S(2)}) copy-start(f32[1024]{0:T(1024)} %get-tuple-element.18) | copy-start | bytes 12292
  393.0 20.7 %copy-start.26 = (f32[1024]{0:T(1024)S(1)}, f32[1024]{0:T(1024)}, u32[]{:S(2)}) copy-start(f32[1024]{0:T(1024)} %get-tuple-element.14) | copy-start | bytes 12292
  393.1 45.3 %copy-start.6 = (f32[1,256,1024]{2,1,0:T(8,128)S(1)}, f32[1,256,1024]{2,1,0:T(8,128)}, u32[]{:S(2)}) copy-start(f32[1,256,1024]{2,1,0:T(8,128)} %copy-done.5) | copy-start | bytes 3145732
  393.1 47.5 %copy-start.1 = (bf16[512,1024]{1,0:T(8,128)(2,1)S(1)}, bf16[512,1024]{1,0:T(8,128)(2,1)}, u32[]{:S(2)}) copy-start(bf16[512,1024]{1,0:T(8,128)(2,1)} %param.26) | copy-start | bytes 3145732
  (25 other events, 213.7 us)
Sparse Core Ops, SparseCore 0:
  13.4 31.4 all-gather.4
  85.6 34.7 reduce-scatter.4
  125.4 27.5 all-gather.6
  154.5 28.6 all-gather.8
  197.5 34.8 reduce-scatter.8
  234.5 33.7 reduce-scatter.6
  273.6 27.5 all-gather.10
  375.7 34.7 reduce-scatter.10
where the time goes:
time: 457 us; the launch traced here: 448 us
  waiting for transfers between devices  214 us (47%)
  matrix products  135 us (30%)
  other arithmetic  49.7 us (11%)
  blocking collectives  24.6 us (5%)
  between operations  15 us (3%)
  local copies, waits for them, and re-layouts  8.62 us (2%)
    reduce_scatter x4, waiting for transfers between devices, seq_reduce(): return lax.psum_scatter(values, 'tp', scatter_dimension=1, tiled=True)  109 us
    all_gather x4, waiting for transfers between devices, seq_gather(): return lax.all_gather(values, 'tp', axis=1, tiled=True)  104 us
    psum x1, blocking collectives, local_step(): grad_ln1_gamma = lax.psum(grad_ln1_gamma, 'tp')  24.6 us
    convert_element_type x1, other arithmetic, local_step(): grad_scores_bf = grad_scores.astype(jnp.bfloat16)  19.7 us
    sub x1, matrix products, local_step(): prob_f = jax.nn.softmax(jnp.where(causal, scores, MASK_VALUE), axis=-1)  19.7 us
    dot_general x1, matrix products, local_step(): jnp.einsum('bhij,bihe->bjhe', prob_bf, grad_context, preferred_element_ty...  13.3 us
    dot_general x1, matrix products, local_step(): jnp.einsum('bihe,bjhe->bhij', grad_context, v_heads, preferred_element_ty...  12.5 us
    dot_general x1, matrix products, local_step(): jnp.einsum('bhij,bjhe->bihe', prob_bf, v_heads, preferred_element_type=jn...  12.3 us
  transfers between devices with their start and end apart: 8, of which 8 were waited for; matrix products, arithmetic and copies ran while one was open for 9% of the time, Pallas kernels for 0%

commit v1 on v0

v1 whole, which is shorter than its diff:
```python
import functools
import math
import jax
import jax.numpy as jnp
import numpy as np
from jax import lax
from jax.experimental import pallas as pl
from jax.experimental.pallas import tpu as pltpu
from jax.sharding import PartitionSpec as P

EPS = 1e-5
MASK_VALUE = -1e30
BF, F32 = jnp.bfloat16, jnp.float32
VMEM = pltpu.VMEM
MESH = pl.DeviceIdType.MESH
VLIM = 62 * 1024 * 1024
GELU_C = math.sqrt(2.0 / math.pi)
PAIR = LOW, HIGH = (0, 1)
TRIPLE = (0, 1, 2)
NN = (((1,), (0,)), ((), ()))
T0 = (((0,), (0,)), ((), ()))
NT = (((1,), (1,)), ((), ()))


def alibi_slopes(n_heads):
    closest = 2 ** int(math.floor(math.log2(n_heads)))
    base_ratio = 2.0 ** (-8.0 / closest)
    extra_ratio = 2.0 ** (-4.0 / closest)
    remaining = min(closest, n_heads - closest)
    slopes = [base_ratio ** (i + 1) for i in range(closest)]
    slopes = slopes + [extra_ratio ** (2 * i + 1) for i in range(remaining)]
    return np.array(slopes, dtype=np.float32)


def mm(a, b, dims=NN):
    return lax.dot_general(a, b, dims, preferred_element_type=F32)


def loop(lo, hi, body, unroll=1):
    def step(i, carry):
        body(i)
        return carry
    lax.fori_loop(lo, hi, step, 0, unroll=unroll)


def rows_loop(total, rows, body, unroll=1):
    loop(0, total // rows, lambda r: body(pl.ds(pl.multiple_of(r * rows, rows), rows)), unroll)


def row_mean(z):
    return jnp.mean(z, axis=-1, keepdims=True)


def col_sum(z):
    return jnp.sum(z, axis=0, keepdims=True)


def norm_back(grad, hat, rstd):
    return rstd * (grad - row_mean(grad) - hat * row_mean(grad * hat))


def zero_fill(*refs):
    for ref in refs:
        ref[...] = jnp.zeros(ref.shape, ref.dtype)


def sort_weight(wp, wt):
    e = wp.shape[0] // 6
    for part_no in TRIPLE:
        for head in PAIR:
            dst = (part_no * 2 + head) * e
            src = (head * 3 + part_no) * e
            wp[dst:dst + e, :] = wt[src:src + e, :]


def norm_rows(z):
    cen = z - row_mean(z)
    rstd = lax.rsqrt(row_mean(cen * cen) + EPS)
    return cen * rstd, rstd


def fold8(v, op):
    out = v[0:8]
    for k in range(1, v.shape[0] // 8):
        out = op(out, v[8 * k:8 * k + 8])
    return out


class Ring:
    def __init__(self, n):
        self.n = n
        nx = n // 2
        self.me = lax.axis_index('tp')
        self.x = self.me // 2
        self.c = self.me % 2
        self.nx = nx
        self.xr = (self.x + 1) % nx
        self.xl = (self.x + nx - 1) % nx
        self.xf = (self.x + 2) % nx
        self.right = self.xr * 2 + self.c
        self.left = self.xl * 2 + self.c
        self.far = self.xf * 2 + self.c
        self.partner = self.x * 2 + (1 - self.c)

    def order(self, s):
        odd = s % 2
        dx = jnp.where(s < 2, 0, jnp.where(s >= 6, 2, jnp.where(odd == 0, self.nx - 1, 1)))
        mid = jnp.where(s < 4, 0, 1)
        dc = jnp.where(s < 2, odd, jnp.where(s >= 6, odd, mid))
        return ((self.x + dx) % self.nx) * 2 + (self.c + dc) % 2

    def barrier(self, everyone=False):
        sem = pltpu.get_barrier_semaphore()
        if everyone:
            peers = [(self.me + k) % self.n for k in range(1, self.n)]
        else:
            peers = [self.right, self.left, self.partner]
        for peer in peers:
            pl.semaphore_signal(sem, inc=1, device_id={'tp': peer}, device_id_type=MESH)
        pl.semaphore_wait(sem, len(peers))


class Gather:
    SENDS = 14

    def __init__(self, ring, buf, ssem, rsem):
        self.ring, self.buf, self.ssem, self.rsem = ring, buf, ssem, rsem
        self.half = buf.shape[1] // 2

    def cp(self, blk, half, dev, k):
        ref = self.buf.at[blk, pl.ds(half * self.half, self.half)]
        return pltpu.make_async_remote_copy(
            src_ref=ref, dst_ref=ref, send_sem=self.ssem.at[k], recv_sem=self.rsem.at[blk, half],
            device_id={'tp': dev}, device_id_type=MESH)

    def start(self):
        r = self.ring
        self.cp(r.me, LOW, r.right, 0).start()
        self.cp(r.me, HIGH, r.left, 1).start()
        self.cp(r.me, HIGH, r.right, 2).start()
        self.cp(r.me, LOW, r.left, 3).start()
        self.cp(r.me, LOW, r.partner, 4).start()
        self.cp(r.me, HIGH, r.partner, 5).start()

    def wait(self, blk, half):
        self.cp(blk, half, self.ring.me, 0).wait_recv()

    def wait_block(self, blk):
        for half in PAIR:
            self.wait(blk, half)

    def near1(self):
        r = self.ring
        self.wait(r.left, LOW)
        self.cp(r.left, LOW, r.right, 6).start()
        self.cp(r.left, LOW, r.partner, 7).start()
        self.wait(r.right, HIGH)
        self.cp(r.right, HIGH, r.left, 8).start()
        self.cp(r.right, HIGH, r.partner, 9).start()

    def near2(self):
        r = self.ring
        self.wait(r.left, HIGH)
        self.cp(r.left, HIGH, r.partner, 10).start()
        self.wait(r.right, LOW)
        self.cp(r.right, LOW, r.partner, 11).start()

    def far(self):
        r = self.ring
        self.wait(r.far, LOW)
        self.cp(r.far, LOW, r.partner, 12).start()
        self.wait(r.far, HIGH)
        self.cp(r.far, HIGH, r.partner, 13).start()

    def finish(self):
        for k in range(self.SENDS):
            self.cp(self.ring.me, 0, self.ring.right, k).wait_send()

    def run(self, body, after_near=None):
        r = self.ring

        def step(s):
            blk = r.order(s)

            @pl.when(s == 1)
            def _():
                self.wait_block(blk)

            @pl.when(s == 2)
            def _():
                self.near1()
                if after_near is not None:
                    after_near()
                self.near2()

            @pl.when((s == 4) | (s == 5) | (s == 7))
            def _():
                self.wait_block(blk)

            @pl.when(s == 6)
            def _():
                self.far()

            body(blk)

        loop(0, r.n, step)


class Scatter:
    SENDS = 10

    def __init__(self, ring, part, pair, stage, land, ssem, rsem):
        self.ring, self.part, self.pair, self.stage, self.land = ring, part, pair, stage, land
        self.ssem, self.rsem = ssem, rsem
        self.rows = part.shape[1]
        self.half = self.rows // 2

    def cp_pair(self, xp, k):
        r = self.ring
        return pltpu.make_async_remote_copy(
            src_ref=self.part.at[xp * 2 + (1 - r.c)], dst_ref=self.pair.at[xp], send_sem=self.ssem.at[k],
            recv_sem=self.rsem.at[xp], device_id={'tp': r.partner}, device_id_type=MESH)

    def cp(self, slot, half, dst_slot, dev, k):
        rows = pl.ds(half * self.half, self.half)
        return pltpu.make_async_remote_copy(
            src_ref=self.stage.at[slot, rows], dst_ref=self.land.at[dst_slot, rows],
            send_sem=self.ssem.at[k], recv_sem=self.rsem.at[4 + 2 * dst_slot + half],
            device_id={'tp': dev}, device_id_type=MESH)

    def wait_land(self, dst_slot, half):
        self.cp(0, half, dst_slot, self.ring.me, 0).wait_recv()

    def wait_pair(self, xp):
        self.cp_pair(xp, 0).wait_recv()

    def send_pair(self, xp, k):
        self.cp_pair(xp, k).start()

    def mix(self, slot, xp, half, with_far=False):
        blk = xp * 2 + self.ring.c
        step = 16

        def body(i):
            rows = pl.ds(pl.multiple_of(half * self.half + i * step, step), step)
            total = self.part[blk, rows, :].astype(F32) + self.pair[xp, rows, :].astype(F32)
            if with_far:
                total = total + self.land[0, rows, :].astype(F32)
            self.stage[slot, rows, :] = total.astype(BF)
        loop(0, self.half // step, body)

    def far(self):
        r = self.ring
        self.wait_pair(r.xf)
        self.mix(0, r.xf, 0)
        self.cp(0, 0, 0, r.right, 4).start()
        self.mix(0, r.xf, 1)
        self.cp(0, 1, 0, r.left, 5).start()

    def near_own(self):
        r = self.ring
        self.wait_pair(r.xr)
        self.mix(1, r.xr, 1)
        self.cp(1, 1, 1, r.right, 6).start()
        self.wait_pair(r.xl)
        self.mix(2, r.xl, 0)
        self.cp(2, 0, 2, r.left, 7).start()

    def near_sum(self):
        r = self.ring
        self.wait_land(0, 0)
        self.mix(1, r.xr, 0, with_far=True)
        self.cp(1, 0, 1, r.right, 8).start()
        self.wait_land(0, 1)
        self.mix(2, r.xl, 1, with_far=True)
        self.cp(2, 1, 2, r.left, 9).start()

    def wait_final(self):
        self.wait_pair(self.ring.x)
        for slot in (1, 2):
            for half in PAIR:
                self.wait_land(slot, half)

    def total(self, rows):
        r = self.ring
        return (self.part[r.me, rows, :].astype(F32) + self.pair[r.x, rows, :].astype(F32)
                + self.land[1, rows, :].astype(F32) + self.land[2, rows, :].astype(F32))

    def finish(self):
        for k in range(4):
            self.cp_pair(self.ring.x, k).wait_send()
        for k in range(4, self.SENDS):
            self.cp(0, 0, 0, self.ring.right, k).wait_send()


def scatter_scratch(n, rows, d):
    return [VMEM((n // 2, rows, d), BF), VMEM((3, rows, d), BF), VMEM((3, rows, d), BF),
            pltpu.SemaphoreType.DMA((Scatter.SENDS,)), pltpu.SemaphoreType.DMA((4 + 6,))]


def gather_scratch(n):
    return [pltpu.SemaphoreType.DMA((Gather.SENDS,)), pltpu.SemaphoreType.DMA((n, 2))]


def lane_mask(rows, h):
    lane = lax.broadcasted_iota(jnp.int32, (rows, 128), 1)
    return (lane < 64) if h == 0 else (lane >= 64)


def attend_block(i, q_ref, k_ref, v_ref, o_ref, lse_ref, s_ref, m_ref, l_ref, acc_ref, slopes, scale):
    t = q_ref.shape[2]
    key = lax.broadcasted_iota(jnp.int32, (t, t), 0)
    qry = lax.broadcasted_iota(jnp.int32, (t, t), 1)
    for h in PAIR:
        m_ref[h] = jnp.full((8, t), MASK_VALUE, F32)
        l_ref[h] = jnp.zeros((8, t), F32)
    zero_fill(acc_ref)

    def score(j, diag):
        pos = (key + j * t).astype(F32)
        for h in PAIR:
            s = mm(k_ref[j], q_ref[h, i], NT) * scale + slopes[h] * pos
            if diag:
                s = jnp.where(key <= qry, s, MASK_VALUE)
            s_ref[h, j] = s
            m_ref[h] = jnp.maximum(m_ref[h], fold8(s, jnp.maximum))

    loop(0, i, lambda j: score(j, False))
    score(i, True)
    top = [jnp.max(m_ref[h], axis=0, keepdims=True) for h in (0, 1)]

    def denom(j):
        for h in PAIR:
            l_ref[h] = l_ref[h] + fold8(jnp.exp(s_ref[h, j] - top[h]), jnp.add)

    loop(0, i + 1, denom)
    for h in PAIR:
        lse_ref[h, i] = top[h] + jnp.log(col_sum(l_ref[h]))

    def values(j):
        total = acc_ref[...]
        for h in PAIR:
            p = jnp.exp(s_ref[h, j] - lse_ref[h, i]).astype(BF)
            total = total + mm(p, v_ref[h, j], T0)
        acc_ref[...] = total

    loop(0, i + 1, values)
    o_ref[i] = acc_ref[...].astype(BF)


def kernel_a(n, scale, x_hbm, dy_hbm, g1, b1, wt, bqkv, wo, bo, g2, b2, slopes_ref,
             h, dy, q, k, v, o, lse, x1, g,
             xg, wp, s_ref, m_ref, l_ref, acc, part, pair, stage, land, rs_s, rs_r,
             ax_s, ax_r, ay_s, ay_r, local):
    ring = Ring(n)
    me = ring.me
    t = xg.shape[1]
    in_x = pltpu.make_async_copy(x_hbm, xg.at[me], local.at[0])
    in_y = pltpu.make_async_copy(dy_hbm, dy.at[me], local.at[1])
    in_x.start()
    in_y.start()
    ring.barrier()
    in_x.wait()
    gx = Gather(ring, xg, ax_s, ax_r)
    gy = Gather(ring, dy, ay_s, ay_r)
    gx.start()
    in_y.wait()
    sort_weight(wp, wt)

    def project(blk):
        def norm(rows):
            hat, _ = norm_rows(xg[blk, rows, :].astype(F32))
            h[blk, rows, :] = (hat * g1[...] + b1[...]).astype(BF)
        rows_loop(t, 32, norm)
        out = mm(h[blk], wp[...], NT) + bqkv[...]
        out = out.astype(BF)
        zero = jnp.zeros((t, 128), BF)
        for head in PAIR:
            q[head, blk] = jnp.where(lane_mask(t, head), out[:, 0:128], zero)
            v[head, blk] = jnp.where(lane_mask(t, head), out[:, 256:384], zero)
        k[blk] = out[:, 128:256]

    gx.run(project, after_near=gy.start)

    slopes = [slopes_ref[me * 2 + head] for head in PAIR]

    def attend(i):
        attend_block(i, q, k, v, o, lse, s_ref, m_ref, l_ref, acc, slopes, scale)

    def all_blocks(i):
        @pl.when(i == n // 2 + 1)
        def _():
            gy.near1()

        @pl.when(i == n - 1)
        def _():
            gy.near2()
        attend(i)

    loop(0, n, all_blocks)

    rs = Scatter(ring, part, pair, stage, land, rs_s, rs_r)

    def partial(xp, slot):
        for cc in PAIR:
            part[xp * 2 + cc] = mm(o[xp * 2 + cc], wo[...]).astype(BF)
        rs.send_pair(xp, slot)

    partial(ring.xf, 0)
    rs.far()
    partial(ring.xr, 1)
    partial(ring.xl, 2)
    rs.near_own()
    partial(ring.x, 3)
    gy.far()
    rs.near_sum()
    for dx in (ring.x, ring.xl, ring.xr, ring.xf):
        gy.wait_block(dx * 2 + (1 - ring.c))
    rs.wait_final()

    def last(rows):
        a = rs.total(rows).astype(BF).astype(F32)
        mid = xg[me, rows, :].astype(F32) + a + bo[...]
        x1[rows, :] = mid
        hat, _ = norm_rows(mid)
        g[rows, :] = (hat * g2[...] + b2[...]).astype(BF)
    rows_loop(t, 32, last)
    rs.finish()
    gx.finish()
    gy.finish()


def kernel_b(n, g_hbm, x1, dyo, dy, wu, bu, wd, g2,
             part_m, gwu, gbu, gwd, mid, da, small,
             gg, act, dpre, part, pair, stage, land, rs_s, rs_r, ag_s, ag_r, local):
    ring = Ring(n)
    me = ring.me
    t, d, f = gg.shape[1], gg.shape[2], wu.shape[1]
    in_g = pltpu.make_async_copy(g_hbm, gg.at[me], local.at[0])
    in_g.start()
    ring.barrier()
    in_g.wait()
    ag = Gather(ring, gg, ag_s, ag_r)
    ag.start()
    zero_fill(gbu)

    def mlp(blk):
        pre = mm(gg[blk], wu[...]) + bu[...]
        cot = mm(dy[blk], wd[...], NT).astype(BF).astype(F32)
        sq = pre * pre
        th = jnp.tanh(GELU_C * (pre + 0.044715 * sq * pre))
        cdf = 0.5 * (1.0 + th)
        act[blk] = (pre * cdf).astype(BF)
        slope = cdf + pre * (0.5 * (1.0 - th * th)) * (GELU_C * (1.0 + 3 * 0.044715 * sq))
        dp = cot * slope
        gbu[...] = gbu[...] + fold8(dp, jnp.add)
        dpre[blk] = dp.astype(BF)
        part[blk] = mm(dpre[blk], wu[...], NT).astype(BF)

    ag.run(mlp)
    rs = Scatter(ring, part, pair, stage, land, rs_s, rs_r)
    rs.send_pair(ring.xf, 0)
    rs.send_pair(ring.xr, 1)
    rs.send_pair(ring.xl, 2)
    rs.send_pair(ring.x, 3)
    rs.far()
    rs.near_own()

    def weight_down(i):
        cols = pl.ds(pl.multiple_of(i * 256, 256), 256)
        left = act[:, :, cols].reshape(n * t, 256)
        gwd[cols, :] = mm(left, dy[...].reshape(n * t, d), T0).astype(BF)

    def weight_up(i):
        cols = pl.ds(pl.multiple_of(i * 256, 256), 256)
        left = gg[:, :, cols].reshape(n * t, 256)
        gwu[cols, :] = mm(left, dpre[...].reshape(n * t, f), T0).astype(BF)

    loop(0, f // 256, weight_down)
    loop(0, d // 256, weight_up)
    rs.near_sum()

    def down(blk):
        part_m[blk] = mm(act[blk], wd[...]).astype(BF)
    loop(0, n, down)
    rs.wait_final()
    zero_fill(small)

    def last(rows):
        dg = rs.total(rows).astype(BF).astype(F32)
        hat, rstd = norm_rows(x1[rows, :])
        small[0] = small[0] + fold8(dg * hat, jnp.add)
        small[1] = small[1] + fold8(dg, jnp.add)
        dh = dg * g2[...]
        dz = norm_back(dh, hat, rstd)
        dyf = dyo[rows, :].astype(F32)
        dm = dyf + dz
        small[2] = small[2] + fold8(dm, jnp.add)
        small[3] = small[3] + fold8(dyf, jnp.add)
        mid[rows, :] = dm
        da[rows, :] = dm.astype(BF)
    rows_loop(t, 16, last)
    rs.finish()
    ag.finish()


def kernel_c(n, scale, da_hbm, mid, part_m, x_own, x1, h, q, k, v, o, lse, wt, wo, g1, bd, small_b, slopes_ref,
             y, gx, sums, gwt, gbq, gwo,
             dag, wp, km, dom, dlt, dq, dk_acc, dv_acc, d3, gwo_acc, small, every,
             part, pair, stage, land, rs_s, rs_r,
             pair_m, stage_m, land_m, rm_s, rm_r, ag_s, ag_r, ar_s, ar_r, local):
    ring = Ring(n)
    me = ring.me
    t, d = dag.shape[1], dag.shape[2]
    in_d = pltpu.make_async_copy(da_hbm, dag.at[me], local.at[0])
    in_d.start()
    ring.barrier(everyone=True)
    in_d.wait()
    ag = Gather(ring, dag, ag_s, ag_r)
    ag.start()
    rm = Scatter(ring, part_m, pair_m, stage_m, land_m, rm_s, rm_r)
    for slot, xp in enumerate((ring.xf, ring.xr, ring.xl, ring.x)):
        rm.send_pair(xp, slot)
    sort_weight(wp, wt)
    zero_fill(gwo_acc)

    def back_out(blk):
        dc = mm(dag[blk], wo[...], NT).astype(BF)
        zero = jnp.zeros((t, 128), BF)
        for head in PAIR:
            mask = lane_mask(t, head)
            dom[head, blk] = jnp.where(mask, dc, zero)
            km[head, blk] = jnp.where(mask, k[blk], zero)
        prod = (dc.astype(F32) * o[blk].astype(F32)).T
        dlt[LOW, blk] = col_sum(prod[:64])
        dlt[HIGH, blk] = col_sum(prod[64:])
        gwo_acc[...] = gwo_acc[...] + mm(o[blk], dag[blk], T0)
        dq[blk] = jnp.zeros((t, 128), F32)

    ag.run(back_out, after_near=rm.far)
    rm.near_own()
    gwo[...] = gwo_acc[...].astype(BF)
    slopes = [slopes_ref[me * 2 + head] for head in PAIR]
    key = lax.broadcasted_iota(jnp.int32, (t, t), 0)
    qry = lax.broadcasted_iota(jnp.int32, (t, t), 1)

    def kv_block(j):
        pos = (key + j * t).astype(F32)
        zero_fill(dk_acc, dv_acc)

        def pair_block(i, diag):
            tv, tk, tq = dv_acc[...], dk_acc[...], dq[i]
            for head in PAIR:
                s = mm(k[j], q[head, i], NT) * scale + slopes[head] * pos
                if diag:
                    s = jnp.where(key <= qry, s, MASK_VALUE)
                p = jnp.exp(s - lse[head, i])
                dp = mm(v[head, j], dom[head, i], NT).astype(BF).astype(F32)
                ds = (p * (dp - dlt[head, i])).astype(BF)
                tv = tv + mm(p.astype(BF), dom[head, i])
                tk = tk + mm(ds, q[head, i])
                tq = tq + mm(ds, km[head, j], T0)
            dv_acc[...] = tv
            dk_acc[...] = tk
            dq[i] = tq

        pair_block(j, True)
        loop(j + 1, n, lambda i: pair_block(i, False))
        d3[j, :, 128:256] = (dk_acc[...] * scale).astype(BF)
        d3[j, :, 256:384] = dv_acc[...].astype(BF)

        @pl.when(j == 1)
        def _():
            rm.near_sum()

    loop(0, n, kv_block)
    zero_fill(gbq)
    rs = Scatter(ring, part, pair, stage, land, rs_s, rs_r)

    def back_in(xp, slot):
        for cc in PAIR:
            blk = xp * 2 + cc
            d3[blk, :, 0:128] = (dq[blk] * scale).astype(BF)
            part[blk] = mm(d3[blk], wp[...]).astype(BF)
        rs.send_pair(xp, slot)

    back_in(ring.xf, 0)
    rs.far()
    back_in(ring.xr, 1)
    back_in(ring.xl, 2)
    rs.near_own()
    back_in(ring.x, 3)

    def weight_in(i):
        cols = pl.ds(pl.multiple_of(i * 128, 128), 128)
        left = d3[:, :, cols].reshape(n * t, 128)
        grad = mm(left, h[...].reshape(n * t, d), T0).astype(BF)
        for head in PAIR:
            gwt[head, i] = grad[head * 64:head * 64 + 64]
    loop(0, 3, weight_in)

    def bias_in(b):
        gbq[...] = gbq[...] + fold8(d3[b].astype(F32), jnp.add)
    loop(0, n, bias_in)
    rs.near_sum()
    rm.wait_final()

    def out_y(rows):
        m = rm.total(rows).astype(BF).astype(F32)
        y[rows, :] = (x1[rows, :] + m + bd[...]).astype(BF)
    rows_loop(t, 32, out_y)
    zero_fill(small)
    rs.wait_final()

    def last(rows):
        dh = rs.total(rows).astype(BF).astype(F32)
        hat, rstd = norm_rows(x_own[rows, :].astype(F32))
        small[0] = small[0] + fold8(dh * hat, jnp.add)
        small[1] = small[1] + fold8(dh, jnp.add)
        dn = dh * g1[...]
        dz = norm_back(dn, hat, rstd)
        gx[rows, :] = (mid[rows, :] + dz).astype(BF)
    rows_loop(t, 16, last)
    for i in range(2):
        every[me, i:i + 1, :] = col_sum(small[i])
    for i in range(4):
        every[me, 2 + i:3 + i, :] = col_sum(small_b[i])
    every[me, 6:8, :] = jnp.zeros((2, d), F32)

    def share(off):
        dev = (me + off) % n
        return pltpu.make_async_remote_copy(
            src_ref=every.at[me], dst_ref=every.at[me], send_sem=ar_s.at[off], recv_sem=ar_r.at[me],
            device_id={'tp': dev}, device_id_type=MESH)

    for off in range(1, n):
        share(off).start()
    for off in range(1, n):
        src = (me + off) % n
        pltpu.make_async_remote_copy(
            src_ref=every.at[src], dst_ref=every.at[src], send_sem=ar_s.at[0], recv_sem=ar_r.at[src],
            device_id={'tp': me}, device_id_type=MESH).wait_recv()
    total = every[0]
    for b in range(1, n):
        total = total + every[b]
    sums[...] = total
    for off in range(1, n):
        share(off).wait_send()
    rs.finish()
    rm.finish()
    ag.finish()


def whole():
    return pl.BlockSpec(memory_space=VMEM)


def anywhere():
    return pl.BlockSpec(memory_space=pl.ANY)


def smem():
    return pl.BlockSpec(memory_space=pltpu.SMEM)


def solution(mesh):
    n = mesh.shape['tp']

    def local_step(x, ln1_gamma, ln1_beta, w_qkv, b_qkv, w_out, b_out, ln2_gamma, ln2_beta, w_up, b_up, w_down, b_down, grad_y):
        t, d = x.shape[1], x.shape[2]
        heads, e = w_qkv.shape[1], w_qkv.shape[3]
        he = heads * e
        f = w_up.shape[1]
        scale = e ** -0.5
        slopes = jnp.asarray(alibi_slopes(heads * n))
        x2, dy2 = x[0], grad_y[0]
        row = lambda vec: vec.reshape(1, -1)
        wt = w_qkv.transpose(1, 2, 3, 0).reshape(heads * 3 * e, d)
        bq = b_qkv.transpose(1, 0, 2).reshape(1, 3 * he)
        sds = jax.ShapeDtypeStruct
        rows, full, half = (t, d), (n, t, d), (n, t, he)
        both, line = (len(PAIR),) + half, (len(PAIR), n, 1, t)
        packed = (len(TRIPLE) * he, d)
        params = lambda cid: pltpu.CompilerParams(collective_id=cid, has_side_effects=True, vmem_limit_bytes=VLIM)
        dma = pltpu.SemaphoreType.DMA

        h, dy, q, k, v, o, lse, x1, g = pl.pallas_call(
            functools.partial(kernel_a, n, scale),
            name='attend_forward',
            out_shape=[sds(full, BF), sds(full, BF), sds(both, BF), sds(half, BF),
                       sds(both, BF), sds(half, BF), sds(line, F32), sds(rows, F32),
                       sds(rows, BF)],
            in_specs=[anywhere(), anywhere()] + [whole()] * 8 + [smem()],
            out_specs=[whole()] * 9,
            scratch_shapes=[VMEM(full, BF), VMEM(packed, BF), VMEM((2, n, t, t), F32), VMEM((2, 8, t), F32),
                            VMEM((2, 8, t), F32), VMEM((t, he), F32), VMEM(full, BF)]
            + scatter_scratch(n, t, d) + gather_scratch(n) + gather_scratch(n) + [dma((2,))],
            compiler_params=params(0),
        )(x2, dy2, row(ln1_gamma), row(ln1_beta), wt, bq, w_out, row(b_out), row(ln2_gamma), row(ln2_beta), slopes)

        part_m, gwu, gbu, gwd, mid, da, small = pl.pallas_call(
            functools.partial(kernel_b, n),
            name='mlp_both',
            out_shape=[sds(full, BF), sds((d, f), BF), sds((8, f), F32), sds((f, d), BF), sds(rows, F32),
                       sds(rows, BF), sds((4, 8, d), F32)],
            in_specs=[anywhere()] + [whole()] * 7,
            out_specs=[whole()] * 7,
            scratch_shapes=[VMEM(full, BF), VMEM((n, t, f), BF), VMEM((n, t, f), BF), VMEM(full, BF)]
            + scatter_scratch(n, t, d) + gather_scratch(n) + [dma((1,))],
            compiler_params=params(1),
        )(g, x1, dy2, dy, w_up, row(b_up), w_down, row(ln2_gamma))

        y, gx, sums, gwt, gbq, gwo = pl.pallas_call(
            functools.partial(kernel_c, n, scale),
            name='attend_backward',
            out_shape=[sds(rows, BF), sds(rows, BF), sds((8, d), F32), sds((heads, 3, e, d), BF),
                       sds((8, 3 * he), F32), sds((he, d), BF)],
            in_specs=[anywhere()] + [whole()] * 15 + [smem()],
            out_specs=[whole()] * 6,
            scratch_shapes=[VMEM(full, BF), VMEM(packed, BF), VMEM(both, BF), VMEM(both, BF),
                            VMEM(line, F32), VMEM(half, F32), VMEM((t, he), F32), VMEM((t, he), F32),
                            VMEM((n, t, 3 * he), BF), VMEM((he, d), F32), VMEM((2, 8, d), F32), VMEM((n, 8, d), F32),
                            VMEM(full, BF)]
            + scatter_scratch(n, t, d) + scatter_scratch(n, t, d) + gather_scratch(n)
            + [dma((n,)), dma((n,)), dma((1,))],
            compiler_params=params(2),
        )(da, mid, part_m, x2, x1, h, q, k, v, o, lse, wt, w_out, row(ln1_gamma), row(b_down), small, slopes)

        s_g1, s_b1, s_g2, s_b2, s_bo, s_bd = list(sums)[:6]
        grad_w_qkv = gwt.transpose(3, 0, 1, 2)
        grad_b_qkv = jnp.sum(gbq, axis=0).reshape(3, heads, e).transpose(1, 0, 2)
        grad_b_up = jnp.sum(gbu, axis=0)
        return (y[None], gx[None], s_g1, s_b1, grad_w_qkv, grad_b_qkv, gwo, s_bo,
                s_g2, s_b2, gwu, grad_b_up, gwd, s_bd)

    row_spec = P('dp', 'tp', None)
    in_specs = (row_spec, P(), P(), P(None, 'tp', None, None), P('tp', None, None), P('tp', None), P(), P(), P(),
                P(None, 'tp'), P('tp'), P('tp', None), P(), row_spec)
    out_specs = (row_spec, row_spec, P('dp'), P('dp'), P('dp', 'tp', None, None), P(('dp', 'tp'), None, None),
                 P(('dp', 'tp'), None), P('dp'), P('dp'), P('dp'), P('dp', 'tp'), P(('dp', 'tp')), P(('dp', 'tp'), None), P('dp'))
    return jax.shard_map(local_step, mesh=mesh, in_specs=in_specs, out_specs=out_specs, check_vma=False)
```

time: 457 us -> 247 us (0.54)
  the two profiles are of different devices: /device:TPU:80 before, /device:TPU:81 now
where the time goes in v1:
time: 247 us; the launch traced here: 246 us
  Pallas kernels  231 us (94%)
  local copies, waits for them, and re-layouts  13 us (5%)
    pallas_call x1, Pallas kernels, local_step(): pl.pallas_call(functools.partial(kernel_c, n, scale), name='attend_backwa...  91.4 us
    pallas_call x1, Pallas kernels, local_step(): pl.pallas_call(functools.partial(kernel_a, n, scale), name='attend_forwar...  84.4 us
    pallas_call x1, Pallas kernels, local_step(): pl.pallas_call(functools.partial(kernel_b, n), name='mlp_both', out_shape...  55 us
    unnamed x12, local copies, waits for them, and re-layouts  9.45 us

profile of v1, /device:TPU:81, one launch (start us, length us, event | category | flops | bytes accessed | tf_op | source)
XLA Modules:
  0.0 246.1 jit_solution(17802435923160346814)
XLA Ops:
  0.6 1.3 reshape.63.bqkv
  2.0 84.4 %attend_forward.1 = (bf16[8,256,1024]{2,1,0:T(8,128)(2,1)}, bf16[8,256,1024]{2,1,0:T(8,128)(2,1)}, bf16[2,8,256,128]{3,2,1,0:T(8,128)(2,1)}, bf16[8,256,128]{2,1...) custom-call(bf16[256,1024]{1,0:T(8,128)(2,1)} %bitcast.27, ...), custom_call_target="tpu_custom_call" | custom-call | tf_op jit(solution)/shard_map/attend_forward/pallas_call | solution.py:687
  86.4 55.0 %mlp_both.1 = (bf16[8,256,1024]{2,1,0:T(8,128)(2,1)}, bf16[1024,512]{1,0:T(8,128)(2,1)}, f32[8,512]{1,0:T(8,128)}, bf16[512,1024]{1,0:T(8,128)(2,1)}, f32[256,10...) custom-call(bf16[256,1024]{1,0:T(8,128)(2,1)} %get-tuple-element.36.g_hbm, ...), custom_call_target="tpu_custom_call" | custom-call | tf_op jit(solution)/shard_map/mlp_both/pallas_call | solution.py:701
  141.4 0.0 copy-start.2
  141.5 91.4 %attend_backward.1 = (bf16[256,1024]{1,0:T(8,128)(2,1)}, bf16[256,1024]{1,0:T(8,128)(2,1)}, f32[8,1024]{1,0:T(8,128)}, bf16[2,3,64,1024]{3,2,1,0:T(8,128)(2,1)},...) custom-call(bf16[256,1024]{1,0:T(8,128)(2,1)} %get-tuple-element.39.da_hbm, f32[256,1024]{1,0:T(8,128)} %get-tuple-element.40.mid, ...), custom_call_target="tpu_custom_call" | custom-call | tf_op jit(solution)/shard_map/attend_backward/pallas_call | solution.py:713
  232.9 0.0 copy-start.1
  232.9 0.0 copy-start
  232.9 0.9 reduce_sum.18
  233.8 0.0 copy-done.2
  233.8 0.6 reduce_sum.19
  234.4 0.7 reshape.69
  235.1 1.6 fusion
  236.7 1.9 copy.35
  238.5 1.9 copy.36
  240.4 2.1 copy.37
  242.5 1.7 copy.38
  244.2 0.0 copy-done.1
  244.2 1.0 copy.39
  245.1 0.0 copy-done
  245.1 1.0 copy.40
Async XLA Ops:
  141.4 92.4 %copy-start.2 = (f32[8,512]{1,0:T(8,128)S(1)}, f32[8,512]{1,0:T(8,128)}, u32[]{:S(2)}) copy-start(f32[8,512]{1,0:T(8,128)} %get-tuple-element.56) | copy-start | bytes 49156
  232.9 11.3 %copy-start.1 = (bf16[1024,512]{1,0:T(8,128)(2,1)S(1)}, bf16[1024,512]{1,0:T(8,128)(2,1)}, u32[]{:S(2)}) copy-start(bf16[1024,512]{1,0:T(8,128)(2,1)} %get-tuple-element.88) | copy-start | bytes 3145732
  232.9 12.2 %copy-start = (bf16[512,1024]{1,0:T(8,128)(2,1)S(1)}, bf16[512,1024]{1,0:T(8,128)(2,1)}, u32[]{:S(2)}) copy-start(bf16[512,1024]{1,0:T(8,128)(2,1)} %get-tuple-element.90) | copy-start | bytes 3145732

commit v2 on v1

--- a/solution.py
+++ b/solution.py
@@ -13,6 +13,7 @@
 BF, F32 = jnp.bfloat16, jnp.float32
 VMEM = pltpu.VMEM
 MESH = pl.DeviceIdType.MESH
+scope = jax.named_scope
 VLIM = 62 * 1024 * 1024
 GELU_C = math.sqrt(2.0 / math.pi)
 PAIR = LOW, HIGH = (0, 1)
@@ -367,12 +368,14 @@
     in_y.wait()
     sort_weight(wp, wt)
 
+    bias = jnp.concatenate([bqkv[part_no, head:head + 1, :] for part_no in TRIPLE for head in PAIR], axis=1)
+
     def project(blk):
         def norm(rows):
             hat, _ = norm_rows(xg[blk, rows, :].astype(F32))
             h[blk, rows, :] = (hat * g1[...] + b1[...]).astype(BF)
         rows_loop(t, 32, norm)
-        out = mm(h[blk], wp[...], NT) + bqkv[...]
+        out = mm(h[blk], wp[...], NT) + bias
         out = out.astype(BF)
         zero = jnp.zeros((t, 128), BF)
         for head in PAIR:
@@ -380,7 +383,8 @@
             v[head, blk] = jnp.where(lane_mask(t, head), out[:, 256:384], zero)
         k[blk] = out[:, 128:256]
 
-    gx.run(project, after_near=gy.start)
+    with scope('a_gather'):
+        gx.run(project, after_near=gy.start)
 
     slopes = [slopes_ref[me * 2 + head] for head in PAIR]
 
@@ -397,7 +401,8 @@
             gy.near2()
         attend(i)
 
-    loop(0, n, all_blocks)
+    with scope('a_attend'):
+        loop(0, n, all_blocks)
 
     rs = Scatter(ring, part, pair, stage, land, rs_s, rs_r)
 
@@ -406,17 +411,22 @@
             part[xp * 2 + cc] = mm(o[xp * 2 + cc], wo[...]).astype(BF)
         rs.send_pair(xp, slot)
 
-    partial(ring.xf, 0)
-    rs.far()
-    partial(ring.xr, 1)
-    partial(ring.xl, 2)
-    rs.near_own()
-    partial(ring.x, 3)
-    gy.far()
-    rs.near_sum()
+    with scope('a_far'):
+        partial(ring.xf, 0)
+        rs.far()
+    with scope('a_own'):
+        partial(ring.xr, 1)
+        partial(ring.xl, 2)
+        rs.near_own()
+        partial(ring.x, 3)
+    with scope('a_gyfar'):
+        gy.far()
+    with scope('a_sum'):
+        rs.near_sum()
     for dx in (ring.x, ring.xl, ring.xr, ring.xf):
         gy.wait_block(dx * 2 + (1 - ring.c))
-    rs.wait_final()
+    with scope('a_final'):
+        rs.wait_final()
 
     def last(rows):
         a = rs.total(rows).astype(BF).astype(F32)
@@ -457,14 +467,17 @@
         dpre[blk] = dp.astype(BF)
         part[blk] = mm(dpre[blk], wu[...], NT).astype(BF)
 
-    ag.run(mlp)
+    with scope('b_gather'):
+        ag.run(mlp)
     rs = Scatter(ring, part, pair, stage, land, rs_s, rs_r)
     rs.send_pair(ring.xf, 0)
     rs.send_pair(ring.xr, 1)
     rs.send_pair(ring.xl, 2)
     rs.send_pair(ring.x, 3)
-    rs.far()
-    rs.near_own()
+    with scope('b_far'):
+        rs.far()
+    with scope('b_own'):
+        rs.near_own()
 
     def weight_down(i):
         cols = pl.ds(pl.multiple_of(i * 256, 256), 256)
@@ -476,14 +489,18 @@
         left = gg[:, :, cols].reshape(n * t, 256)
         gwu[cols, :] = mm(left, dpre[...].reshape(n * t, f), T0).astype(BF)
 
-    loop(0, f // 256, weight_down)
-    loop(0, d // 256, weight_up)
-    rs.near_sum()
+    with scope('b_weights'):
+        loop(0, f // 256, weight_down)
+        loop(0, d // 256, weight_up)
+    with scope('b_sum'):
+        rs.near_sum()
 
     def down(blk):
         part_m[blk] = mm(act[blk], wd[...]).astype(BF)
-    loop(0, n, down)
-    rs.wait_final()
+    with scope('b_down'):
+        loop(0, n, down)
+    with scope('b_final'):
+        rs.wait_final()
     zero_fill(small)
 
     def last(rows):
@@ -537,8 +554,10 @@
         gwo_acc[...] = gwo_acc[...] + mm(o[blk], dag[blk], T0)
         dq[blk] = jnp.zeros((t, 128), F32)
 
-    ag.run(back_out, after_near=rm.far)
-    rm.near_own()
+    with scope('c_gather'):
+        ag.run(back_out, after_near=rm.far)
+    with scope('c_mown'):
+        rm.near_own()
     gwo[...] = gwo_acc[...].astype(BF)
     slopes = [slopes_ref[me * 2 + head] for head in PAIR]
     key = lax.broadcasted_iota(jnp.int32, (t, t), 0)
@@ -573,7 +592,8 @@
         def _():
             rm.near_sum()
 
-    loop(0, n, kv_block)
+    with scope('c_attend'):
+        loop(0, n, kv_block)
     zero_fill(gbq)
     rs = Scatter(ring, part, pair, stage, land, rs_s, rs_r)
 
@@ -584,12 +604,14 @@
             part[blk] = mm(d3[blk], wp[...]).astype(BF)
         rs.send_pair(xp, slot)
 
-    back_in(ring.xf, 0)
-    rs.far()
-    back_in(ring.xr, 1)
-    back_in(ring.xl, 2)
-    rs.near_own()
-    back_in(ring.x, 3)
+    with scope('c_far'):
+        back_in(ring.xf, 0)
+        rs.far()
+    with scope('c_own'):
+        back_in(ring.xr, 1)
+        back_in(ring.xl, 2)
+        rs.near_own()
+        back_in(ring.x, 3)
 
     def weight_in(i):
         cols = pl.ds(pl.multiple_of(i * 128, 128), 128)
@@ -597,20 +619,24 @@
         grad = mm(left, h[...].reshape(n * t, d), T0).astype(BF)
         for head in PAIR:
             gwt[head, i] = grad[head * 64:head * 64 + 64]
-    loop(0, 3, weight_in)
+    with scope('c_weights'):
+        loop(0, len(TRIPLE), weight_in)
 
     def bias_in(b):
         gbq[...] = gbq[...] + fold8(d3[b].astype(F32), jnp.add)
     loop(0, n, bias_in)
-    rs.near_sum()
-    rm.wait_final()
+    with scope('c_sum'):
+        rs.near_sum()
+    with scope('c_mfinal'):
+        rm.wait_final()
 
     def out_y(rows):
         m = rm.total(rows).astype(BF).astype(F32)
         y[rows, :] = (x1[rows, :] + m + bd[...]).astype(BF)
     rows_loop(t, 32, out_y)
     zero_fill(small)
-    rs.wait_final()
+    with scope('c_final'):
+        rs.wait_final()
 
     def last(rows):
         dh = rs.total(rows).astype(BF).astype(F32)
@@ -633,8 +659,9 @@
             src_ref=every.at[me], dst_ref=every.at[me], send_sem=ar_s.at[off], recv_sem=ar_r.at[me],
             device_id={'tp': dev}, device_id_type=MESH)
 
-    for off in range(1, n):
-        share(off).start()
+    with scope('c_share'):
+        for off in range(1, n):
+            share(off).start()
     for off in range(1, n):
         src = (me + off) % n
         pltpu.make_async_remote_copy(
@@ -651,6 +678,31 @@
     ag.finish()
 
 
+def kernel_out(n_big, *refs):
+    srcs, (gbq, gbu, sums), refs = refs[:n_big], refs[n_big:n_big + 3], refs[n_big + 3:]
+    outs, (o_bq, o_bu), refs = refs[:n_big], refs[n_big:n_big + 2], refs[n_big + 2:]
+    o_sums, refs = refs[:6], refs[6:]
+    bufs, (sem_in, sem_out) = refs[:n_big], refs[n_big:]
+    ins = [pltpu.make_async_copy(a, b, sem_in.at[i]) for i, (a, b) in enumerate(zip(srcs, bufs))]
+    backs = [pltpu.make_async_copy(b, a, sem_out.at[i]) for i, (a, b) in enumerate(zip(outs, bufs))]
+    for cp in ins:
+        cp.start()
+    o_bu[...] = col_sum(gbu[...])
+    row = col_sum(gbq[...])
+    e = o_bq.shape[2]
+    for part_no in TRIPLE:
+        for head in PAIR:
+            at = (part_no * 2 + head) * e
+            o_bq[part_no, head:head + 1, :] = row[:, at:at + e]
+    for i, ref in enumerate(o_sums):
+        ref[...] = sums[i:i + 1, :]
+    for cp, back in zip(ins, backs):
+        cp.wait()
+        back.start()
+    for back in backs:
+        back.wait()
+
+
 def whole():
     return pl.BlockSpec(memory_space=VMEM)
 
@@ -676,7 +728,7 @@
         x2, dy2 = x[0], grad_y[0]
         row = lambda vec: vec.reshape(1, -1)
         wt = w_qkv.transpose(1, 2, 3, 0).reshape(heads * 3 * e, d)
-        bq = b_qkv.transpose(1, 0, 2).reshape(1, 3 * he)
+        bq = b_qkv.transpose(1, 0, 2)
         sds = jax.ShapeDtypeStruct
         rows, full, half = (t, d), (n, t, d), (n, t, he)
         both, line = (len(PAIR),) + half, (len(PAIR), n, 1, t)
@@ -726,12 +778,20 @@
             compiler_params=params(2),
         )(da, mid, part_m, x2, x1, h, q, k, v, o, lse, wt, w_out, row(ln1_gamma), row(b_down), small, slopes)
 
-        s_g1, s_b1, s_g2, s_b2, s_bo, s_bd = list(sums)[:6]
-        grad_w_qkv = gwt.transpose(3, 0, 1, 2)
-        grad_b_qkv = jnp.sum(gbq, axis=0).reshape(3, heads, e).transpose(1, 0, 2)
-        grad_b_up = jnp.sum(gbu, axis=0)
-        return (y[None], gx[None], s_g1, s_b1, grad_w_qkv, grad_b_qkv, gwo, s_bo,
-                s_g2, s_b2, gwu, grad_b_up, gwd, s_bd)
+        big = (y, gx, gwt, gwo, gwu, gwd)
+        res = pl.pallas_call(
+            functools.partial(kernel_out, len(big)),
+            name='results',
+            out_shape=[sds(b.shape, b.dtype) for b in big] + [sds((len(TRIPLE), heads, e), F32), sds((1, f), F32)]
+            + [sds((1, d), F32)] * 6,
+            in_specs=[anywhere()] * len(big) + [whole()] * 3,
+            out_specs=[anywhere()] * len(big) + [whole()] * 8,
+            scratch_shapes=[VMEM(b.shape, b.dtype) for b in big] + [dma((len(big),))] * 2,
+        )(*big, gbq, gbu, sums)
+        y, gx, gwt, gwo, gwu, gwd, gbq, gbu, s_g1, s_b1, s_g2, s_b2, s_bo, s_bd = res
+        vec = lambda a: a.reshape(-1)
+        return (y[None], gx[None], vec(s_g1), vec(s_b1), gwt.transpose(3, 0, 1, 2), gbq.transpose(1, 0, 2), gwo, vec(s_bo),
+                vec(s_g2), vec(s_b2), gwu, vec(gbu), gwd, vec(s_bd))
 
     row_spec = P('dp', 'tp', None)
     in_specs = (row_spec, P(), P(), P(None, 'tp', None, None), P('tp', None, None), P('tp', None), P(), P(), P(),

time: 247 us -> 237 us (0.960)
  local copies, waits for them, and re-layouts: 13 us -> 0 us
  Pallas kernels: 231 us -> 236 us
    unnamed x12 -> x0, local copies, waits for them, and re-layouts: 9.45 us -> none
    pallas_call x0 -> x1, Pallas kernels: none -> 5.16 us  [local_step(): pl.pallas_call(functools.partial(kernel_out, len(big)), name='results', o...]
where the time goes in v2:
time: 237 us
  Pallas kernels  236 us (100%)
    pallas_call x1, Pallas kernels, local_step(): pl.pallas_call(functools.partial(kernel_c, n, scale), name='attend_backwa...  91.4 us
    pallas_call x1, Pallas kernels, local_step(): pl.pallas_call(functools.partial(kernel_a, n, scale), name='attend_forwar...  84.4 us
    pallas_call x1, Pallas kernels, local_step(): pl.pallas_call(functools.partial(kernel_b, n), name='mlp_both', out_shape...  55.1 us
    pallas_call x1, Pallas kernels, local_step(): pl.pallas_call(functools.partial(kernel_out, len(big)), name='results', o...  5.16 us

profile of v2, /device:TPU:81, one launch (start us, length us, event | category | flops | bytes accessed | tf_op | source)
XLA Modules:
  0.0 236.7 jit_solution(2566662505560762866)
XLA Ops:
  0.6 84.4 %attend_forward.1 = (bf16[8,256,1024]{2,1,0:T(8,128)(2,1)}, bf16[8,256,1024]{2,1,0:T(8,128)(2,1)}, bf16[2,8,256,128]{3,2,1,0:T(8,128)(2,1)}, bf16[8,256,128]{2,1...) custom-call(bf16[256,1024]{1,0:T(8,128)(2,1)} %bitcast.28, ...), custom_call_target="tpu_custom_call" | custom-call | tf_op jit(solution)/shard_map/attend_forward/pallas_call | solution.py:739
  85.0 55.1 %mlp_both.1 = (bf16[8,256,1024]{2,1,0:T(8,128)(2,1)}, bf16[1024,512]{1,0:T(8,128)(2,1)}, f32[8,512]{1,0:T(8,128)}, bf16[512,1024]{1,0:T(8,128)(2,1)}, f32[256,10...) custom-call(bf16[256,1024]{1,0:T(8,128)(2,1)} %get-tuple-element.50.g_hbm, ...), custom_call_target="tpu_custom_call" | custom-call | tf_op jit(solution)/shard_map/mlp_both/pallas_call | solution.py:753
  140.1 91.4 %attend_backward.1 = (bf16[256,1024]{1,0:T(8,128)(2,1)}, bf16[256,1024]{1,0:T(8,128)(2,1)}, f32[8,1024]{1,0:T(8,128)}, bf16[2,3,64,1024]{3,2,1,0:T(8,128)(2,1)},...) custom-call(bf16[256,1024]{1,0:T(8,128)(2,1)} %get-tuple-element.53.da_hbm, f32[256,1024]{1,0:T(8,128)} %get-tuple-element.54.mid, ...), custom_call_target="tpu_custom_call" | custom-call | tf_op jit(solution)/shard_map/attend_backward/pallas_call | solution.py:765
  231.5 5.2 %results.1 = (bf16[256,1024]{1,0:T(8,128)(2,1)}, bf16[256,1024]{1,0:T(8,128)(2,1)}, bf16[2,3,64,1024]{3,2,1,0:T(8,128)(2,1)}, bf16[128,1024]{1,0:T(8,128)(2,1)},...) custom-call(bf16[256,1024]{1,0:T(8,128)(2,1)} %get-tuple-element.63., ...), custom_call_target="tpu_custom_call" | custom-call | tf_op jit(solution)/shard_map/results/pallas_call | solution.py:782

commit v3 on v2

--- a/solution.py
+++ b/solution.py
@@ -349,113 +349,112 @@
     o_ref[i] = acc_ref[...].astype(BF)
 
 
-def kernel_a(n, scale, x_hbm, dy_hbm, g1, b1, wt, bqkv, wo, bo, g2, b2, slopes_ref,
-             h, dy, q, k, v, o, lse, x1, g,
-             xg, wp, s_ref, m_ref, l_ref, acc, part, pair, stage, land, rs_s, rs_r,
-             ax_s, ax_r, ay_s, ay_r, local):
+def kernel_main(n, scale, x_hbm, dy_hbm, wt_hbm, wo_hbm, wu_hbm, wd_hbm, g1, b1, bqkv, bo, g2, b2, bu, bd, slopes_ref,
+                y, gx, sums, gwt, gbq, gwo, gwu, gbu, gwd, h_hbm,
+                xg, xo, dyo, dy, hg, wt, wp, wof, wu, wd, q, k, v, o, lse, orow, s_ref, m_ref, l_ref, acc,
+                x1, act, dpre, mid, dcs, dcr, km, dom, dlt, dq, dk_acc, dv_acc, d3, small, every, part,
+                *rest):
+    rest = list(rest)
+
+    def take(count):
+        head = rest[:count]
+        del rest[:count]
+        return head
+
     ring = Ring(n)
     me = ring.me
-    t = xg.shape[1]
-    in_x = pltpu.make_async_copy(x_hbm, xg.at[me], local.at[0])
-    in_y = pltpu.make_async_copy(dy_hbm, dy.at[me], local.at[1])
-    in_x.start()
-    in_y.start()
-    ring.barrier()
+    t, d, f = xg.shape[1], xg.shape[2], wu.shape[1]
+    rs_refs, rm_refs = take(5), take(5)
+    ax, ay, aw, ag, ad = [Gather(ring, buf, *take(2)) for buf in (xg, dy, wof, hg, xg)]
+    o_send, o_recv, c_send, c_recv, ar_s, ar_r, local = take(7)
+
+    def fetch(i, src, dst):
+        cp = pltpu.make_async_copy(src, dst, local.at[i])
+        cp.start()
+        return cp
+
+    in_x, in_wo, in_dy, in_wt = (fetch(0, x_hbm, xg.at[me]), fetch(1, wo_hbm, wof.at[me]),
+                                 fetch(2, dy_hbm, dy.at[me]), fetch(3, wt_hbm, wt))
+    later = [fetch(4, wu_hbm, wu), fetch(5, wd_hbm, wd), fetch(6, x_hbm, xo), fetch(7, dy_hbm, dyo)]
+    ring.barrier(everyone=True)
     in_x.wait()
-    gx = Gather(ring, xg, ax_s, ax_r)
-    gy = Gather(ring, dy, ay_s, ay_r)
-    gx.start()
-    in_y.wait()
+    ax.start()
+    in_wt.wait()
     sort_weight(wp, wt)
-
-    bias = jnp.concatenate([bqkv[part_no, head:head + 1, :] for part_no in TRIPLE for head in PAIR], axis=1)
+    in_wo.wait()
+    in_dy.wait()
+    bias = jnp.concatenate([bqkv[kind, head:head + 1, :] for kind in TRIPLE for head in PAIR], axis=1)
 
     def project(blk):
         def norm(rows):
             hat, _ = norm_rows(xg[blk, rows, :].astype(F32))
-            h[blk, rows, :] = (hat * g1[...] + b1[...]).astype(BF)
+            hg[blk, rows, :] = (hat * g1[...] + b1[...]).astype(BF)
         rows_loop(t, 32, norm)
-        out = mm(h[blk], wp[...], NT) + bias
+        out = mm(hg[blk], wp[...], NT) + bias
         out = out.astype(BF)
         zero = jnp.zeros((t, 128), BF)
         for head in PAIR:
-            q[head, blk] = jnp.where(lane_mask(t, head), out[:, 0:128], zero)
-            v[head, blk] = jnp.where(lane_mask(t, head), out[:, 256:384], zero)
+            q[head, blk] = jnp.where(lane_mask(t, head), out[:, :128], zero)
+            v[head, blk] = jnp.where(lane_mask(t, head), out[:, 256:], zero)
         k[blk] = out[:, 128:256]
+        fetch(0, hg.at[blk], h_hbm.at[blk])
 
     with scope('a_gather'):
-        gx.run(project, after_near=gy.start)
-
+        ax.run(project, after_near=aw.start)
     slopes = [slopes_ref[me * 2 + head] for head in PAIR]
 
-    def attend(i):
+    def send_o(i):
+        cols = pl.ds(pl.multiple_of(me * 128, 128), 128)
+        return pltpu.make_async_remote_copy(
+            src_ref=o.at[i], dst_ref=orow.at[:, cols], send_sem=o_send.at[i], recv_sem=o_recv.at[me],
+            device_id={'tp': i}, device_id_type=MESH)
+
+    def all_blocks(i):
+        for at, act_now in ((2, aw.near2), (3, aw.far), (n - 2, ay.near1), (n - 1, ay.near2)):
+            pl.when(i == at)(act_now)
         attend_block(i, q, k, v, o, lse, s_ref, m_ref, l_ref, acc, slopes, scale)
 
-    def all_blocks(i):
-        @pl.when(i == n // 2 + 1)
+        @pl.when(i != me)
         def _():
-            gy.near1()
-
-        @pl.when(i == n - 1)
-        def _():
-            gy.near2()
-        attend(i)
+            send_o(i).start()
 
     with scope('a_attend'):
+        aw.near1()
+        ay.start()
+        ax.finish()
+        pltpu.make_async_copy(hg, h_hbm, local.at[0]).wait()
         loop(0, n, all_blocks)
-
-    rs = Scatter(ring, part, pair, stage, land, rs_s, rs_r)
-
-    def partial(xp, slot):
-        for cc in PAIR:
-            part[xp * 2 + cc] = mm(o[xp * 2 + cc], wo[...]).astype(BF)
-        rs.send_pair(xp, slot)
-
-    with scope('a_far'):
-        partial(ring.xf, 0)
-        rs.far()
-    with scope('a_own'):
-        partial(ring.xr, 1)
-        partial(ring.xl, 2)
-        rs.near_own()
-        partial(ring.x, 3)
-    with scope('a_gyfar'):
-        gy.far()
-    with scope('a_sum'):
-        rs.near_sum()
-    for dx in (ring.x, ring.xl, ring.xr, ring.xf):
-        gy.wait_block(dx * 2 + (1 - ring.c))
-    with scope('a_final'):
-        rs.wait_final()
-
-    def last(rows):
-        a = rs.total(rows).astype(BF).astype(F32)
-        mid = xg[me, rows, :].astype(F32) + a + bo[...]
-        x1[rows, :] = mid
-        hat, _ = norm_rows(mid)
-        g[rows, :] = (hat * g2[...] + b2[...]).astype(BF)
-    rows_loop(t, 32, last)
-    rs.finish()
-    gx.finish()
-    gy.finish()
-
-
-def kernel_b(n, g_hbm, x1, dyo, dy, wu, bu, wd, g2,
-             part_m, gwu, gbu, gwd, mid, da, small,
-             gg, act, dpre, part, pair, stage, land, rs_s, rs_r, ag_s, ag_r, local):
-    ring = Ring(n)
-    me = ring.me
-    t, d, f = gg.shape[1], gg.shape[2], wu.shape[1]
-    in_g = pltpu.make_async_copy(g_hbm, gg.at[me], local.at[0])
-    in_g.start()
-    ring.barrier()
-    in_g.wait()
-    ag = Gather(ring, gg, ag_s, ag_r)
-    ag.start()
-    zero_fill(gbu)
+    with scope('a_wait'):
+        orow[:, pl.ds(pl.multiple_of(me * 128, 128), 128)] = o[me]
+        for off in range(1, n):
+            src = (me + off) % n
+            cols = pl.ds(pl.multiple_of(src * 128, 128), 128)
+            pltpu.make_async_remote_copy(
+                src_ref=o.at[0], dst_ref=orow.at[:, cols], send_sem=o_send.at[0], recv_sem=o_recv.at[src],
+                device_id={'tp': me}, device_id_type=MESH).wait_recv()
+        for dx in (ring.x, ring.xl, ring.xr, ring.xf):
+            aw.wait_block(dx * 2 + (1 - ring.c))
+        later[2].wait()
+    with scope('a_out'):
+        x1[...] = mm(orow[...], wof[...].reshape(n * 128, d)).astype(BF).astype(F32)
+
+        def enter(rows):
+            row = xo[rows, :].astype(F32) + x1[rows, :] + bo[...]
+            x1[rows, :] = row
+            hat, _ = norm_rows(row)
+            hg[me, rows, :] = (hat * g2[...] + b2[...]).astype(BF)
+        rows_loop(t, 32, enter)
+        ag.start()
+    with scope('a_rest'):
+        ay.far()
+        for dx in (ring.x, ring.xl, ring.xr, ring.xf):
+            ay.wait_block(dx * 2 + (1 - ring.c))
+        for cp in (later[0], later[1], later[3]):
+            cp.wait()
+        zero_fill(gbu)
 
     def mlp(blk):
-        pre = mm(gg[blk], wu[...]) + bu[...]
+        pre = mm(hg[blk], wu[...]) + bu[...]
         cot = mm(dy[blk], wd[...], NT).astype(BF).astype(F32)
         sq = pre * pre
         th = jnp.tanh(GELU_C * (pre + 0.044715 * sq * pre))
@@ -469,15 +468,15 @@
 
     with scope('b_gather'):
         ag.run(mlp)
-    rs = Scatter(ring, part, pair, stage, land, rs_s, rs_r)
-    rs.send_pair(ring.xf, 0)
-    rs.send_pair(ring.xr, 1)
-    rs.send_pair(ring.xl, 2)
-    rs.send_pair(ring.x, 3)
+    rs = Scatter(ring, part, *rs_refs)
+    chips = (ring.xf, ring.xr, ring.xl, ring.x)
+    for slot, xp in enumerate(chips):
+        rs.send_pair(xp, slot)
     with scope('b_far'):
         rs.far()
     with scope('b_own'):
         rs.near_own()
+    ay.finish()
 
     def weight_down(i):
         cols = pl.ds(pl.multiple_of(i * 256, 256), 256)
@@ -486,7 +485,7 @@
 
     def weight_up(i):
         cols = pl.ds(pl.multiple_of(i * 256, 256), 256)
-        left = gg[:, :, cols].reshape(n * t, 256)
+        left = hg[:, :, cols].reshape(n * t, 256)
         gwu[cols, :] = mm(left, dpre[...].reshape(n * t, f), T0).astype(BF)
 
     with scope('b_weights'):
@@ -494,55 +493,62 @@
         loop(0, d // 256, weight_up)
     with scope('b_sum'):
         rs.near_sum()
+    zero_fill(small)
 
     def down(blk):
-        part_m[blk] = mm(act[blk], wd[...]).astype(BF)
+        dy[blk] = mm(act[blk], wd[...]).astype(BF)
     with scope('b_down'):
         loop(0, n, down)
     with scope('b_final'):
         rs.wait_final()
-    zero_fill(small)
-
-    def last(rows):
+
+    def leave(rows):
         dg = rs.total(rows).astype(BF).astype(F32)
         hat, rstd = norm_rows(x1[rows, :])
-        small[0] = small[0] + fold8(dg * hat, jnp.add)
-        small[1] = small[1] + fold8(dg, jnp.add)
-        dh = dg * g2[...]
-        dz = norm_back(dh, hat, rstd)
+        small[2] = small[2] + fold8(dg * hat, jnp.add)
+        small[3] = small[3] + fold8(dg, jnp.add)
+        dz = norm_back(dg * g2[...], hat, rstd)
         dyf = dyo[rows, :].astype(F32)
         dm = dyf + dz
-        small[2] = small[2] + fold8(dm, jnp.add)
-        small[3] = small[3] + fold8(dyf, jnp.add)
+        small[4] = small[4] + fold8(dm, jnp.add)
+        small[5] = small[5] + fold8(dyf, jnp.add)
         mid[rows, :] = dm
-        da[rows, :] = dm.astype(BF)
-    rows_loop(t, 16, last)
-    rs.finish()
-    ag.finish()
-
-
-def kernel_c(n, scale, da_hbm, mid, part_m, x_own, x1, h, q, k, v, o, lse, wt, wo, g1, bd, small_b, slopes_ref,
-             y, gx, sums, gwt, gbq, gwo,
-             dag, wp, km, dom, dlt, dq, dk_acc, dv_acc, d3, gwo_acc, small, every,
-             part, pair, stage, land, rs_s, rs_r,
-             pair_m, stage_m, land_m, rm_s, rm_r, ag_s, ag_r, ar_s, ar_r, local):
-    ring = Ring(n)
-    me = ring.me
-    t, d = dag.shape[1], dag.shape[2]
-    in_d = pltpu.make_async_copy(da_hbm, dag.at[me], local.at[0])
-    in_d.start()
-    ring.barrier(everyone=True)
-    in_d.wait()
-    ag = Gather(ring, dag, ag_s, ag_r)
-    ag.start()
-    rm = Scatter(ring, part_m, pair_m, stage_m, land_m, rm_s, rm_r)
-    for slot, xp in enumerate((ring.xf, ring.xr, ring.xl, ring.x)):
+        xg[me, rows, :] = dm.astype(BF)
+
+    def send_c(dev):
+        return pltpu.make_async_remote_copy(
+            src_ref=dcs.at[dev], dst_ref=dcr.at[me], send_sem=c_send.at[dev], recv_sem=c_recv.at[me],
+            device_id={'tp': dev}, device_id_type=MESH)
+
+    with scope('b_leave'):
+        rows_loop(t, 16, leave)
+        rs.finish()
+        ag.finish()
+    with scope('c_send'):
+        def back_out(step):
+            dev = ring.order(n - 1 - step)
+            dcs[dev] = mm(xg[me], wof[dev], NT).astype(BF)
+
+            @pl.when(step < n - 1)
+            def _():
+                send_c(dev).start()
+        loop(0, n, back_out)
+        ad.start()
+        reload = fetch(0, h_hbm, hg)
+    rm = Scatter(ring, dy, *rm_refs)
+    for slot, xp in enumerate(chips):
         rm.send_pair(xp, slot)
-    sort_weight(wp, wt)
-    zero_fill(gwo_acc)
-
-    def back_out(blk):
-        dc = mm(dag[blk], wo[...], NT).astype(BF)
+    dcr[me] = dcs[me]
+
+    def prepare(step):
+        blk = ring.order(step)
+
+        @pl.when(step > 0)
+        def _():
+            pltpu.make_async_remote_copy(
+                src_ref=dcs.at[0], dst_ref=dcr.at[blk], send_sem=c_send.at[0], recv_sem=c_recv.at[blk],
+                device_id={'tp': me}, device_id_type=MESH).wait_recv()
+        dc = dcr[blk]
         zero = jnp.zeros((t, 128), BF)
         for head in PAIR:
             mask = lane_mask(t, head)
@@ -551,15 +557,11 @@
         prod = (dc.astype(F32) * o[blk].astype(F32)).T
         dlt[LOW, blk] = col_sum(prod[:64])
         dlt[HIGH, blk] = col_sum(prod[64:])
-        gwo_acc[...] = gwo_acc[...] + mm(o[blk], dag[blk], T0)
         dq[blk] = jnp.zeros((t, 128), F32)
 
-    with scope('c_gather'):
-        ag.run(back_out, after_near=rm.far)
-    with scope('c_mown'):
-        rm.near_own()
-    gwo[...] = gwo_acc[...].astype(BF)
-    slopes = [slopes_ref[me * 2 + head] for head in PAIR]
+    with scope('c_prepare'):
+        rm.far()
+        loop(0, n, prepare)
     key = lax.broadcasted_iota(jnp.int32, (t, t), 0)
     qry = lax.broadcasted_iota(jnp.int32, (t, t), 1)
 
@@ -583,24 +585,21 @@
             dk_acc[...] = tk
             dq[i] = tq
 
+        for at, act_now in ((2, ad.near1), (2, rm.near_own), (3, ad.near2), (n - 3, rm.near_sum)):
+            pl.when(j == at)(act_now)
         pair_block(j, True)
         loop(j + 1, n, lambda i: pair_block(i, False))
         d3[j, :, 128:256] = (dk_acc[...] * scale).astype(BF)
-        d3[j, :, 256:384] = dv_acc[...].astype(BF)
-
-        @pl.when(j == 1)
-        def _():
-            rm.near_sum()
+        d3[j, :, 256:] = dv_acc[...].astype(BF)
 
     with scope('c_attend'):
         loop(0, n, kv_block)
     zero_fill(gbq)
-    rs = Scatter(ring, part, pair, stage, land, rs_s, rs_r)
 
     def back_in(xp, slot):
         for cc in PAIR:
             blk = xp * 2 + cc
-            d3[blk, :, 0:128] = (dq[blk] * scale).astype(BF)
+            d3[blk, :, :128] = (dq[blk] * scale).astype(BF)
             part[blk] = mm(d3[blk], wp[...]).astype(BF)
         rs.send_pair(xp, slot)
 
@@ -612,21 +611,29 @@
         back_in(ring.xl, 2)
         rs.near_own()
         back_in(ring.x, 3)
+    with scope('c_da'):
+        ad.far()
+        reload.wait()
 
     def weight_in(i):
         cols = pl.ds(pl.multiple_of(i * 128, 128), 128)
         left = d3[:, :, cols].reshape(n * t, 128)
-        grad = mm(left, h[...].reshape(n * t, d), T0).astype(BF)
+        grad = mm(left, hg[...].reshape(n * t, d), T0).astype(BF)
         for head in PAIR:
             gwt[head, i] = grad[head * 64:head * 64 + 64]
+
+    def bias_in(b):
+        gbq[...] = gbq[...] + fold8(d3[b].astype(F32), jnp.add)
+
     with scope('c_weights'):
         loop(0, len(TRIPLE), weight_in)
-
-    def bias_in(b):
-        gbq[...] = gbq[...] + fold8(d3[b].astype(F32), jnp.add)
-    loop(0, n, bias_in)
+        loop(0, n, bias_in)
     with scope('c_sum'):
         rs.near_sum()
+    with scope('c_gwo'):
+        for dx in (ring.x, ring.xl, ring.xr, ring.xf):
+            ad.wait_block(dx * 2 + (1 - ring.c))
+        gwo[...] = mm(o[...].reshape(n * t, 128), xg[...].reshape(n * t, d), T0).astype(BF)
     with scope('c_mfinal'):
         rm.wait_final()
 
@@ -634,48 +641,44 @@
         m = rm.total(rows).astype(BF).astype(F32)
         y[rows, :] = (x1[rows, :] + m + bd[...]).astype(BF)
     rows_loop(t, 32, out_y)
-    zero_fill(small)
     with scope('c_final'):
         rs.wait_final()
 
     def last(rows):
         dh = rs.total(rows).astype(BF).astype(F32)
-        hat, rstd = norm_rows(x_own[rows, :].astype(F32))
+        hat, rstd = norm_rows(xo[rows, :].astype(F32))
         small[0] = small[0] + fold8(dh * hat, jnp.add)
         small[1] = small[1] + fold8(dh, jnp.add)
-        dn = dh * g1[...]
-        dz = norm_back(dn, hat, rstd)
-        gx[rows, :] = (mid[rows, :] + dz).astype(BF)
-    rows_loop(t, 16, last)
-    for i in range(2):
+        gx[rows, :] = (mid[rows, :] + norm_back(dh * g1[...], hat, rstd)).astype(BF)
+    with scope('c_last'):
+        rows_loop(t, 16, last)
+    for i in range(6):
         every[me, i:i + 1, :] = col_sum(small[i])
-    for i in range(4):
-        every[me, 2 + i:3 + i, :] = col_sum(small_b[i])
-    every[me, 6:8, :] = jnp.zeros((2, d), F32)
+    every[me, 6:, :] = jnp.zeros((2, d), F32)
 
     def share(off):
-        dev = (me + off) % n
         return pltpu.make_async_remote_copy(
             src_ref=every.at[me], dst_ref=every.at[me], send_sem=ar_s.at[off], recv_sem=ar_r.at[me],
-            device_id={'tp': dev}, device_id_type=MESH)
+            device_id={'tp': (me + off) % n}, device_id_type=MESH)
 
     with scope('c_share'):
         for off in range(1, n):
             share(off).start()
-    for off in range(1, n):
-        src = (me + off) % n
-        pltpu.make_async_remote_copy(
-            src_ref=every.at[src], dst_ref=every.at[src], send_sem=ar_s.at[0], recv_sem=ar_r.at[src],
-            device_id={'tp': me}, device_id_type=MESH).wait_recv()
-    total = every[0]
-    for b in range(1, n):
-        total = total + every[b]
-    sums[...] = total
+        for off in range(1, n):
+            src = (me + off) % n
+            pltpu.make_async_remote_copy(
+                src_ref=every.at[src], dst_ref=every.at[src], send_sem=ar_s.at[0], recv_sem=ar_r.at[src],
+                device_id={'tp': me}, device_id_type=MESH).wait_recv()
+        total = every[0]
+        for b in range(1, n):
+            total = total + every[b]
+        sums[...] = total
     for off in range(1, n):
         share(off).wait_send()
-    rs.finish()
-    rm.finish()
-    ag.finish()
+        send_o((me + off) % n).wait_send()
+        send_c((me + off) % n).wait_send()
+    for job in (rs, rm, aw, ad):
+        job.finish()
 
 
 def kernel_out(n_big, *refs):
@@ -736,47 +739,26 @@
         params = lambda cid: pltpu.CompilerParams(collective_id=cid, has_side_effects=True, vmem_limit_bytes=VLIM)
         dma = pltpu.SemaphoreType.DMA
 
-        h, dy, q, k, v, o, lse, x1, g = pl.pallas_call(
-            functools.partial(kernel_a, n, scale),
-            name='attend_forward',
-            out_shape=[sds(full, BF), sds(full, BF), sds(both, BF), sds(half, BF),
-                       sds(both, BF), sds(half, BF), sds(line, F32), sds(rows, F32),
-                       sds(rows, BF)],
-            in_specs=[anywhere(), anywhere()] + [whole()] * 8 + [smem()],
-            out_specs=[whole()] * 9,
-            scratch_shapes=[VMEM(full, BF), VMEM(packed, BF), VMEM((2, n, t, t), F32), VMEM((2, 8, t), F32),
-                            VMEM((2, 8, t), F32), VMEM((t, he), F32), VMEM(full, BF)]
-            + scatter_scratch(n, t, d) + gather_scratch(n) + gather_scratch(n) + [dma((2,))],
+        vm = lambda dims, kind=BF: VMEM(dims, kind)
+        stat, square = (len(PAIR), 8, t), (t, he)
+        y, gx, sums, gwt, gbq, gwo, gwu, gbu, gwd, _ = pl.pallas_call(
+            functools.partial(kernel_main, n, scale),
+            name='layer',
+            out_shape=[sds(rows, BF), sds(rows, BF), sds((8, d), F32), sds((heads, len(TRIPLE), e, d), BF),
+                       sds((8, len(TRIPLE) * he), F32), sds((he, d), BF), sds((d, f), BF), sds((8, f), F32),
+                       sds((f, d), BF), sds(full, BF)],
+            in_specs=[anywhere()] * 6 + [whole()] * 8 + [smem()],
+            out_specs=[whole()] * 9 + [anywhere()],
+            scratch_shapes=[vm(full), vm(rows), vm(rows), vm(full), vm(full), vm(packed), vm(packed), vm((n, he, d)), vm((d, f)),
+                            vm((f, d)), vm(both), vm(half), vm(both), vm(half), vm(line, F32), vm(rows),
+                            vm((len(PAIR), n, t, t), F32), vm(stat, F32), vm(stat, F32), vm(square, F32),
+                            vm(rows, F32), vm((n, t, f)), vm((n, t, f)), vm(rows, F32), vm(half), vm(half),
+                            vm(both), vm(both), vm(line, F32), vm(half, F32), vm(square, F32), vm(square, F32),
+                            vm((n, t, len(TRIPLE) * he)), vm((6, 8, d), F32), vm((n, 8, d), F32), vm(full)]
+            + scatter_scratch(n, t, d) * 2 + gather_scratch(n) * 5 + [dma((n,))] * 7,
             compiler_params=params(0),
-        )(x2, dy2, row(ln1_gamma), row(ln1_beta), wt, bq, w_out, row(b_out), row(ln2_gamma), row(ln2_beta), slopes)
-
-        part_m, gwu, gbu, gwd, mid, da, small = pl.pallas_call(
-            functools.partial(kernel_b, n),
-            name='mlp_both',
-            out_shape=[sds(full, BF), sds((d, f), BF), sds((8, f), F32), sds((f, d), BF), sds(rows, F32),
-                       sds(rows, BF), sds((4, 8, d), F32)],
-            in_specs=[anywhere()] + [whole()] * 7,
-            out_specs=[whole()] * 7,
-            scratch_shapes=[VMEM(full, BF), VMEM((n, t, f), BF), VMEM((n, t, f), BF), VMEM(full, BF)]
-            + scatter_scratch(n, t, d) + gather_scratch(n) + [dma((1,))],
-            compiler_params=params(1),
-        )(g, x1, dy2, dy, w_up, row(b_up), w_down, row(ln2_gamma))
-
-        y, gx, sums, gwt, gbq, gwo = pl.pallas_call(
-            functools.partial(kernel_c, n, scale),
-            name='attend_backward',
-            out_shape=[sds(rows, BF), sds(rows, BF), sds((8, d), F32), sds((heads, 3, e, d), BF),
-                       sds((8, 3 * he), F32), sds((he, d), BF)],
-            in_specs=[anywhere()] + [whole()] * 15 + [smem()],
-            out_specs=[whole()] * 6,
-            scratch_shapes=[VMEM(full, BF), VMEM(packed, BF), VMEM(both, BF), VMEM(both, BF),
-                            VMEM(line, F32), VMEM(half, F32), VMEM((t, he), F32), VMEM((t, he), F32),
-                            VMEM((n, t, 3 * he), BF), VMEM((he, d), F32), VMEM((2, 8, d), F32), VMEM((n, 8, d), F32),
-                            VMEM(full, BF)]
-            + scatter_scratch(n, t, d) + scatter_scratch(n, t, d) + gather_scratch(n)
-            + [dma((n,)), dma((n,)), dma((1,))],
-            compiler_params=params(2),
-        )(da, mid, part_m, x2, x1, h, q, k, v, o, lse, wt, w_out, row(ln1_gamma), row(b_down), small, slopes)
+        )(x2, dy2, wt, w_out, w_up, w_down, row(ln1_gamma), row(ln1_beta), bq, row(b_out), row(ln2_gamma), row(ln2_beta),
+          row(b_up), row(b_down), slopes)
 
         big = (y, gx, gwt, gwo, gwu, gwd)
         res = pl.pallas_call(

time: 237 us -> 190 us (0.80)
  Pallas kernels: 236 us -> 189 us
    pallas_call x3 -> x1, Pallas kernels: 231 us -> 184 us  [local_step(): pl.pallas_call(functools.partial(kernel_main, n, scale), name='layer', ou...]
where the time goes in v3:
time: 190 us
  Pallas kernels  189 us (99%)
    pallas_call x1, Pallas kernels, local_step(): pl.pallas_call(functools.partial(kernel_main, n, scale), name='layer', ou...  184 us
    pallas_call x1, Pallas kernels, local_step(): pl.pallas_call(functools.partial(kernel_out, len(big)), name='results', o...  5.16 us

profile of v3, /device:TPU:81, one launch (start us, length us, event | category | flops | bytes accessed | tf_op | source)
XLA Modules:
  0.0 189.8 jit_solution(551338064012287195)
XLA Ops:
  0.7 183.9 %layer.1 = (bf16[256,1024]{1,0:T(8,128)(2,1)}, bf16[256,1024]{1,0:T(8,128)(2,1)}, f32[8,1024]{1,0:T(8,128)}, bf16[2,3,64,1024]{3,2,1,0:T(8,128)(2,1)}, f32[8,384...) custom-call(bf16[256,1024]{1,0:T(8,128)(2,1)} %bitcast.25, ...), custom_call_target="tpu_custom_call" | custom-call | tf_op jit(solution)/shard_map/layer/pallas_call | solution.py:744
  184.6 5.2 %results.1 = (bf16[256,1024]{1,0:T(8,128)(2,1)}, bf16[256,1024]{1,0:T(8,128)(2,1)}, bf16[2,3,64,1024]{3,2,1,0:T(8,128)(2,1)}, bf16[128,1024]{1,0:T(8,128)(2,1)},...) custom-call(bf16[256,1024]{1,0:T(8,128)(2,1)} %get-tuple-element.37., ...), custom_call_target="tpu_custom_call" | custom-call | tf_op jit(solution)/shard_map/results/pallas_call | solution.py:764
